TPU v7x, 512 devices: a whole 4x8x8 slice. The times are simulated.
512 devices in a mesh: cell: 8 (over x, core), own: 64 (over y, z).
Axes of the slice: x: 4, y: 8, z: 8, core: 2. Of those that a mesh axis runs over, the one named last changes fastest.
Arguments:
- gaussians: float32 [4096, 9, 128], P(('cell', 'own')), may hold values from -10 to 16, as said below
- fetch_ids: int32 [8, 64, 64, 4], P('cell', 'own'), may hold values from 0 to 511, as said below
- tile_lists: int32 [8, 64, 12], P('cell', 'own'), may hold values from 0 to 255, as said below
- counts: int32 [8, 64], P('cell', 'own'), may hold values from 6 to 12
- cell_rank: int32 [64, 8], P('own'), may hold values from 0 to 7, each once within a row
- d_colour: float32 [64, 3, 256], P('own', None, 'cell'), may hold values from -96 to 96
Outputs:
- colour: float32 [64, 3, 256], P('own', None, 'cell')
- grads: float32 [4096, 9, 128], P(('cell', 'own'))
Inputs may be any that keep to these rules, and one draw needn't show every extreme that they name: `gaussians`: rows of a block along the second dimension: mean x and y in the tile's pixel frame (0 to 16), la and lc (-3 to 0.3), rho (-0.7 to 0.7), logit (-10 to -6), red, green, blue (0 to 1). fetch_ids[c, o, p, :] are 4 different numbers from p * 8 to (p + 1) * 8 - 1. `tile_lists`: each list holds 12 different slots.
All inputs are finite; a program needn't handle non-finite values.
Results may differ from a plain program's by a relative error of at most 0.0003.
Values sent between devices are 32-bit elements; how exact they have to be, the bound alone decides.
A program may use at most 64 MiB of HBM per device.

v0:
```python
import jax
import jax.numpy as jnp
from jax import lax
from jax.sharding import PartitionSpec as P

TILE_SIDE = 16
PIX = 256


exact_prec = lax.Precision.HIGHEST


def render_tile(blocks, live_count):
    list_len = blocks.shape[0]
    gauss_count = blocks.shape[2]
    pixels = jnp.arange(PIX, dtype=jnp.int32)
    across = (pixels % TILE_SIDE).astype(jnp.float32) + 0.5
    pixel_row = (pixels // TILE_SIDE).astype(jnp.float32) + 0.5
    delta_x = across[None, None, :] - blocks[:, 0, :, None]
    delta_y = pixel_row[None, None, :] - blocks[:, 1, :, None]
    inverse_a = jnp.exp(blocks[:, 2, :, None])
    inverse_c = jnp.exp(blocks[:, 3, :, None])
    cross_term = blocks[:, 4, :, None] * jnp.exp(
        0.5 * (blocks[:, 2, :, None] + blocks[:, 3, :, None])
    )
    exponent = (
        0.5 * (inverse_a * delta_x * delta_x + inverse_c * delta_y * delta_y)
        + cross_term * delta_x * delta_y
    )
    live_mask = (jnp.arange(list_len, dtype=jnp.int32) < live_count).astype(jnp.float32)
    opacity = jax.nn.sigmoid(blocks[:, 5, :]) * live_mask[:, None]
    coverage = opacity[:, :, None] * jnp.exp(-exponent)
    log_keep = jnp.log1p(-coverage)
    gauss_order = jnp.arange(gauss_count, dtype=jnp.int32)
    strict = (gauss_order[None, :] < gauss_order[:, None]).astype(jnp.float32)
    within = jnp.einsum("hg,lgp->lhp", strict, log_keep, precision=exact_prec)
    totals = jnp.sum(log_keep, axis=1)
    through = jnp.cumsum(totals, axis=0)
    offsets = through - totals
    weight = jnp.exp(within + offsets[:, None, :]) * coverage
    colour = jnp.einsum("lkg,lgp->kp", blocks[:, 6:9, :], weight, precision=exact_prec)
    return (colour, through[-1])


def body(gaussians, fetch_ids, tile_lists, counts, cell_rank, d_colour):
    owners = lax.axis_size("own")
    held = gaussians.shape[0]
    local_blocks = gaussians.reshape(held, -1)
    per_block = local_blocks.shape[1]
    wanted = lax.all_to_all(
        fetch_ids.reshape(owners, -1), "own", split_axis=0, concat_axis=0, tiled=True
    )
    first_block = lax.axis_index("own") * held
    local_index = wanted.reshape(-1) - first_block
    owner_hit = (local_index[:, None] == jnp.arange(held, dtype=jnp.int32)[None, :]).astype(
        jnp.float32
    )
    outgoing = jnp.dot(owner_hit, local_blocks, precision=exact_prec).reshape(owners, -1, per_block)
    fetched = lax.all_to_all(outgoing, "own", split_axis=0, concat_axis=0, tiled=True).reshape(
        -1, per_block
    )
    tile_slots = tile_lists.reshape(tile_lists.shape[1], tile_lists.shape[2])
    tile_counts = counts.reshape(-1)
    flat_lists = tile_slots.reshape(-1)
    blocks = fetched[flat_lists].reshape(tile_slots.shape[0], tile_slots.shape[1], 9, -1)

    def render_one(tile_args):
        return render_tile(tile_args[0], tile_args[1])

    colour, log_total = lax.map(render_one, (blocks, tile_counts))
    earlier = (cell_rank[:, None, :] < cell_rank[:, :, None]).astype(jnp.float32)
    stacked = jnp.concatenate([colour, log_total[:, None, :]], axis=1)[:, :, None, :]
    exchanged = lax.all_to_all(stacked, "cell", split_axis=3, concat_axis=2, tiled=True)
    part_colour = exchanged[:, :3]
    part_log = exchanged[:, 3]
    shade_log = jnp.einsum("tab,tbp->tap", earlier, part_log, precision=exact_prec)
    lit_cells = jnp.exp(shade_log)
    result = jnp.sum(lit_cells[:, None] * part_colour, axis=2)
    dotted = jnp.sum(part_colour * d_colour[:, :, None, :], axis=1)
    behind_share = jnp.einsum("tba,tbp->tap", earlier, lit_cells * dotted, precision=exact_prec)
    weights = jnp.concatenate(
        [lit_cells[:, None] * d_colour[:, :, None, :], behind_share[:, None]], axis=1
    )
    returned = lax.all_to_all(weights, "cell", split_axis=2, concat_axis=3, tiled=True)
    colour_back = returned[:, :3, 0]
    behind = returned[:, 3, 0]

    def tile_grad(tile_args):
        tile_blocks, live_count, back_colour, back_log = tile_args
        _, pullback = jax.vjp(lambda tile_params: render_tile(tile_params, live_count), tile_blocks)
        return pullback((back_colour, back_log))[0]

    pair_grads = lax.map(tile_grad, (blocks, tile_counts, colour_back, behind))
    slot_hit = (
        flat_lists[:, None] == jnp.arange(fetched.shape[0], dtype=jnp.int32)[None, :]
    ).astype(jnp.float32)
    slot_grads = jnp.einsum(
        "ps,pf->sf", slot_hit, pair_grads.reshape(flat_lists.shape[0], -1), precision=exact_prec
    )
    incoming = lax.all_to_all(
        slot_grads.reshape(owners, -1, per_block), "own", split_axis=0, concat_axis=0, tiled=True
    )
    summed = jnp.einsum(
        "sr,sf->rf", owner_hit, incoming.reshape(-1, per_block), precision=exact_prec
    ).reshape(held, 9, -1)
    return (result, summed)


def solution(mesh):
    in_specs = (
        P(("cell", "own"), None, None),
        P("cell", "own", None, None),
        P("cell", "own", None),
        P("cell", "own"),
        P("own", None),
        P("own", None, "cell"),
    )
    out_specs = (P("own", None, "cell"), P(("cell", "own"), None, None))
    return jax.shard_map(body, mesh=mesh, in_specs=in_specs, out_specs=out_specs, check_vma=False)
```

profile of v0, /device:TPU:16, one launch (start us, length us, event | category | flops | bytes accessed | tf_op | source)
XLA Modules:
  0.0 154.2 jit_solution(18155211411999824497)
XLA Ops:
  0.6 1.4 copy.39
  2.0 16.5 %all-to-all-start = ((s32[64,1,4]{2,1,0:T(1,128)}), s32[64,1,4]{2,1,0:T(1,128)S(1)}, u32[]{:S(2)}, u32[]{:S(2)}) async-start(s32[64,1,4]{2,1,0:T(1,128)} %bitcast.1), calls=%async_computation | async-start | bytes 65536 | tf_op jit(solution)/shard_map/all_to_all | solution.py:50
  18.5 10.1 %all-to-all-done = s32[64,1,4]{2,1,0:T(1,128)S(1)} async-done(((s32[64,1,4]{2,1,0:T(1,128)}), s32[64,1,4]{2,1,0:T(1,128)S(1)}, u32[]{:S(2)}, u32[]{:S(2)}) %all-to-all-start) | async-done | bytes 1056 | tf_op jit(solution)/shard_map/all_to_all | solution.py:50
  28.7 0.5 broadcast.348
  29.2 0.7 fusion.88
  30.0 0.7 fusion.50
  30.7 1.8 %copy.41 = f32[64,4,1152]{2,1,0:T(4,128)} copy(f32[64,4,1152]{2,0,1:T(8,128)S(1)} %fusion.50) | data formatting | bytes 2359296 | tf_op jit(solution)/shard_map/dot_general | solution.py:58
  32.5 6.6 %all-to-all-start.1 = ((f32[64,4,1152]{2,1,0:T(4,128)}), f32[64,4,1152]{2,1,0:T(4,128)S(1)}, u32[]{:S(2)}, u32[]{:S(2)}) async-start(f32[64,4,1152]{2,1,0:T(4,128)} %copy.41), calls=%async_computation.1 | async-start | bytes 2359296 | tf_op jit(solution)/shard_map/all_to_all | solution.py:59
  39.7 31.3 %all-to-all-done.1 = f32[64,4,1152]{2,1,0:T(4,128)S(1)} async-done(((f32[64,4,1152]{2,1,0:T(4,128)}), f32[64,4,1152]{2,1,0:T(4,128)S(1)}, u32[]{:S(2)}, u32[]{:S(2)}) %all-to-all-start.1) | async-done | bytes 1179680 | tf_op jit(solution)/shard_map/all_to_all | solution.py:59
  71.0 0.4 reshape.388
  71.4 0.6 gather_fusion
  72.1 0.1 bitcast_multiply_fusion.5
  72.2 1.4 log-plus-one_reduce_fusion
  73.7 2.1 %add_exponential_fusion = f32[12,256,128]{2,1,0:T(8,128)S(1)} fusion(f32[12,256]{1,0:T(8,128)S(1)} %sub.144, f32[12,128]{1,0:T(8,128)S(1)} %get-tuple-element.67, f32[12,128]{1,0:T(8,128)S(1)} %get-tuple-element.68, f32[256]{0:T(256)S(1)} %get-tuple-element.71, f32[12,128]{1,0:T(8,128)S(1)} %get-tuple-element.69, f32[12,128]{1,0:T(8,128)S(1)} %get-tuple-element.70, ...), kind=kOutput, calls=%fused_computation.55 | convolution fusion | flops 609894400 | bytes 1624064 | tf_op jit(solution)/shard_map/while/body/eval_jaxpr/hg,lgp->lhp/dot_general | solution.py:36
  75.9 2.0 %convolution_bitcast_fusion.2 = f32[1,3,256]{2,1,0:T(4,128)S(1)} fusion(f32[12,256,128]{2,1,0:T(8,128)S(1)} %add_exponential_fusion, f32[12,128]{1,0:T(8,128)S(1)} %get-tuple-element.67, f32[12,128]{1,0:T(8,128)S(1)} %get-tuple-element.68, f32[256]{0:T(256)S(1)} %get-tuple-element.71, f32[12,128]{1,0:T(8,128)S(1)} %get-tuple-element.69, ...), kind=kOutput, calls=%fused_computation.63 | convolution fusion | flops 19660800 | bytes 1651712 | tf_op jit(solution)/shard_map/while/body/eval_jaxpr/lkg,lgp->kp/dot_general | solution.py:41
  77.9 0.1 copy.43
  78.0 0.5 broadcast.352
  78.5 1.0 reduce.7
  79.5 0.7 reshape.416
  80.2 4.3 %all-to-all-start.2 = ((f32[8,1,128]{2,1,0:T(1,128)}), f32[8,1,128]{2,1,0:T(1,128)S(1)}, u32[]{:S(2)}, u32[]{:S(2)}) async-start(f32[8,1,128]{2,1,0:T(1,128)} %reshape.416), calls=%async_computation.2 | async-start | bytes 8192 | tf_op jit(solution)/shard_map/all_to_all | solution.py:73
  84.5 5.2 %all-to-all-done.2 = f32[8,1,128]{2,1,0:T(1,128)S(1)} async-done(((f32[8,1,128]{2,1,0:T(1,128)}), f32[8,1,128]{2,1,0:T(1,128)S(1)}, u32[]{:S(2)}, u32[]{:S(2)}) %all-to-all-start.2) | async-done | bytes 4128 | tf_op jit(solution)/shard_map/all_to_all | solution.py:73
  89.7 0.7 reduce.8
  90.4 0.2 reshape.417
  90.6 0.1 slice.84
  90.7 0.1 copy.66
  90.8 0.1 copy.65
  91.0 0.2 convolution_exponential_fusion
  91.2 0.3 convolution_bitcast_fusion.1
  91.5 0.7 reshape.418
  92.2 3.5 %all-to-all-start.3 = ((f32[8,1,128]{2,1,0:T(1,128)}), f32[8,1,128]{2,1,0:T(1,128)S(1)}, u32[]{:S(2)}, u32[]{:S(2)}) async-start(f32[8,1,128]{2,1,0:T(1,128)} %reshape.418), calls=%async_computation.3 | async-start | bytes 8192 | tf_op jit(solution)/shard_map/all_to_all | solution.py:84
  95.7 4.9 %all-to-all-done.3 = f32[8,1,128]{2,1,0:T(1,128)S(1)} async-done(((f32[8,1,128]{2,1,0:T(1,128)}), f32[8,1,128]{2,1,0:T(1,128)S(1)}, u32[]{:S(2)}, u32[]{:S(2)}) %all-to-all-start.3) | async-done | bytes 4128 | tf_op jit(solution)/shard_map/all_to_all | solution.py:84
  100.6 0.7 reduce.9
  101.3 0.1 reshape.419
  101.4 0.1 all_to_all.36
  101.5 1.7 %convolution_bitcast_fusion = f32[12,3,128]{2,1,0:T(4,128)S(1)} fusion(f32[12,256,128]{2,1,0:T(8,128)S(1)} %add_exponential_fusion, f32[12,128]{1,0:T(8,128)S(1)} %get-tuple-element.67, f32[12,128]{1,0:T(8,128)S(1)} %get-tuple-element.68, f32[256]{0:T(256)S(1)} %get-tuple-element.71, f32[12,128]{1,0:T(8,128)S(1)} %get-tuple-element.69, ...), kind=kOutput, calls=%fused_computation.60 | convolution fusion | flops 19660800 | bytes 1634304 | tf_op jit(solution)/shard_map/while/body/eval_jaxpr/transpose(jvp(lkg,lgp->kp))/dot_general | solution.py:41
  103.1 2.3 %fusion.30 = (f32[12,256]{1,0:T(8,128)S(1)}, f32[12,128,256]{1,2,0:T(8,128)S(1)}) fusion(f32[12,256,128]{2,1,0:T(8,128)S(1)} %add_exponential_fusion, f32[12,128]{1,0:T(8,128)S(1)} %get-tuple-element.67, f32[12,128]{1,0:T(8,128)S(1)} %get-tuple-element.68, f32[256]{0:T(256)S(1)} %get-tuple-element.71, f32[12,128]{1,0:T(8,128)S(1)} %get-tuple-element.69, ...), kind=kOutput, calls=%fused_computation.52 | convolution fusion | flops 20444160 | bytes 3237888 | tf_op jit(solution)/shard_map/while/body/eval_jaxpr/transpose(jvp(lkg,lgp->kp))/dot_general | solution.py:41
  105.6 4.5 %fusion.24 = (f32[12,128]{1,0:T(8,128)S(1)}, f32[12,128]{1,0:T(8,128)S(1)}, f32[12,128]{1,0:T(8,128)S(1)}, f32[12,128]{1,0:T(8,128)S(1)}, f32[12,128]{1,0:T(8,128)S(1)}, /*index=5*/f32[12,128]{1,0:T(8,128)S(1)}) fusion(f32[12,128]{1,0:T(8,128)S(1)} %get-tuple-element.68, f32[256]{0:T(256)S(1)} %get-tuple-element.71, f32[12,128]{1,0:T(8,128)S(1)} %get-tuple-element.70, ...), kind=kOutput, calls=%fused_computation.42 | convolution fusion | flops 628366336 | bytes 3233792 | tf_op jit(solution)/shard_map/while/body/eval_jaxpr/transpose(jvp(hg,lgp->lhp))/dot_general | solution.py:36
  110.1 0.1 fusion.65
  110.2 0.1 pad_add_fusion
  110.4 0.7 fusion.52
  111.1 1.8 %copy.51 = f32[64,4,1152]{2,1,0:T(4,128)} copy(f32[64,4,1152]{2,0,1:T(8,128)S(1)} %fusion.52) | data formatting | bytes 2359296 | tf_op jit(solution)/shard_map/ps,pf->sf/dot_general | solution.py:97
  112.9 6.3 %all-to-all-start.4 = ((f32[64,4,1152]{2,1,0:T(4,128)}), f32[64,4,1152]{2,1,0:T(4,128)S(1)}, u32[]{:S(2)}, u32[]{:S(2)}) async-start(f32[64,4,1152]{2,1,0:T(4,128)} %copy.51), calls=%async_computation.4 | async-start | bytes 2359296 | tf_op jit(solution)/shard_map/all_to_all | solution.py:100
  119.2 0.1 sub.145
  119.3 0.6 copy.53
  119.8 32.3 %all-to-all-done.4 = f32[64,4,1152]{2,1,0:T(4,128)S(1)} async-done(((f32[64,4,1152]{2,1,0:T(4,128)}), f32[64,4,1152]{2,1,0:T(4,128)S(1)}, u32[]{:S(2)}, u32[]{:S(2)}) %all-to-all-start.4) | async-done | bytes 1179680 | tf_op jit(solution)/shard_map/all_to_all | solution.py:100
  152.2 0.4 reshape.391
  152.6 0.4 copy.52
  152.9 1.3 fusion.63
  (38 shorter events, 0.5 us)
Async XLA Ops:
  0.6 29.4 %copy-start = (f32[8,9,128]{2,0,1:T(8,128)S(1)}, f32[8,9,128]{2,0,1:T(8,128)}, u32[]{:S(2)}) copy-start(f32[8,9,128]{2,0,1:T(8,128)} %param.6) | copy-start | bytes 110596
  2.0 26.6 %all-to-all-start = ((s32[64,1,4]{2,1,0:T(1,128)}), s32[64,1,4]{2,1,0:T(1,128)S(1)}, u32[]{:S(2)}, u32[]{:S(2)}) async-start(s32[64,1,4]{2,1,0:T(1,128)} %bitcast.1), calls=%async_computation | async-start | bytes 65536 | tf_op jit(solution)/shard_map/all_to_all | solution.py:50
  32.5 7.2 %copy-start.2 = (s32[1,1,12]{2,1,0:T(1,128)S(1)}, s32[1,1,12]{2,1,0:T(1,128)}, u32[]{:S(2)}) copy-start(s32[1,1,12]{2,1,0:T(1,128)} %param.8) | copy-start | bytes 148
  32.5 38.6 %all-to-all-start.1 = ((f32[64,4,1152]{2,1,0:T(4,128)}), f32[64,4,1152]{2,1,0:T(4,128)S(1)}, u32[]{:S(2)}, u32[]{:S(2)}) async-start(f32[64,4,1152]{2,1,0:T(4,128)} %copy.41), calls=%async_computation.1 | async-start | bytes 2359296 | tf_op jit(solution)/shard_map/all_to_all | solution.py:59
  75.8 8.7 %copy-start.1 = (f32[1,3,32]{2,0,1:T(1,128)S(1)}, f32[1,3,32]{2,0,1:T(1,128)}, u32[]{:S(2)}) copy-start(f32[1,3,32]{2,0,1:T(1,128)} %param.11) | copy-start | bytes 1156
  75.9 15.1 %copy-start.3 = (s32[1,8]{1,0:T(1,128)S(1)}, s32[1,8]{1,0:T(1,128)}, u32[]{:S(2)}) copy-start(s32[1,8]{1,0:T(1,128)} %param.10) | copy-start | bytes 100
  80.2 9.5 %all-to-all-start.2 = ((f32[8,1,128]{2,1,0:T(1,128)}), f32[8,1,128]{2,1,0:T(1,128)S(1)}, u32[]{:S(2)}, u32[]{:S(2)}) async-start(f32[8,1,128]{2,1,0:T(1,128)} %reshape.416), calls=%async_computation.2 | async-start | bytes 8192 | tf_op jit(solution)/shard_map/all_to_all | solution.py:73
  92.2 8.5 %all-to-all-start.3 = ((f32[8,1,128]{2,1,0:T(1,128)}), f32[8,1,128]{2,1,0:T(1,128)S(1)}, u32[]{:S(2)}, u32[]{:S(2)}) async-start(f32[8,1,128]{2,1,0:T(1,128)} %reshape.418), calls=%async_computation.3 | async-start | bytes 8192 | tf_op jit(solution)/shard_map/all_to_all | solution.py:84
  112.9 39.3 %all-to-all-start.4 = ((f32[64,4,1152]{2,1,0:T(4,128)}), f32[64,4,1152]{2,1,0:T(4,128)S(1)}, u32[]{:S(2)}, u32[]{:S(2)}) async-start(f32[64,4,1152]{2,1,0:T(4,128)} %copy.51), calls=%async_computation.4 | async-start | bytes 2359296 | tf_op jit(solution)/shard_map/all_to_all | solution.py:100
where the time goes:
time: 155 us; the launch traced here: 154 us
  waiting for transfers between devices  83.9 us (54%)
  starting transfers between devices  37.1 us (24%)
  matrix products  15.8 us (10%)
  local copies, waits for them, and re-layouts  10.8 us (7%)
  other arithmetic  5 us (3%)
  between operations  1.65 us (1%)
    all_to_all x1, waiting for transfers between devices, body(): lax.all_to_all(slot_grads.reshape(owners, -1, per_block), 'own', split_ax...  32.3 us
    all_to_all x1, waiting for transfers between devices, body(): lax.all_to_all(outgoing, 'own', split_axis=0, concat_axis=0, tiled=True)  31.3 us
    all_to_all x1, starting transfers between devices, body(): lax.all_to_all(fetch_ids.reshape(owners, -1), 'own', split_axis=0, concat...  16.5 us
    all_to_all x1, waiting for transfers between devices, body(): lax.all_to_all(fetch_ids.reshape(owners, -1), 'own', split_axis=0, concat...  10.1 us
    dot_general x2, matrix products, render_tile(): within = jnp.einsum('hg,lgp->lhp', strict, log_keep, precision=exact_prec)  6.63 us
    all_to_all x1, starting transfers between devices, body(): lax.all_to_all(outgoing, 'own', split_axis=0, concat_axis=0, tiled=True)  6.55 us
    all_to_all x1, starting transfers between devices, body(): lax.all_to_all(slot_grads.reshape(owners, -1, per_block), 'own', split_ax...  6.27 us
    dot_general x3, matrix products, render_tile(): jnp.einsum('lkg,lgp->kp', blocks[:, 6:9, :], weight, precision=exact_prec)  6 us
  transfers between devices with their start and end apart: 5, of which 5 were waited for; matrix products, arithmetic and copies ran while one was open for 0% of the time, Pallas kernels for 0%

commit v1 on v0

v1 whole, which is shorter than its diff:
```python
import jax
import jax.numpy as jnp
from jax import lax
from jax.experimental import pallas as pl
from jax.experimental.pallas import tpu as pltpu
from jax.sharding import PartitionSpec as P

MESH = pl.DeviceIdType.MESH
F32 = jnp.float32
BF16 = jnp.bfloat16

LIST = 12
CAP = 4
OWN = 64
CELL = 8
BLK = 8
GP = 128
NPX = 4
L_PEER, L_RANK, L_BLK, L_DCOL = 0, 16, 32, 64


def iota(shape, dim):
    return lax.broadcasted_iota(jnp.int32, shape, dim)


def split(x):
    hi = x.astype(BF16)
    return hi, (x - hi.astype(F32)).astype(BF16)


def mm(a, b):
    return lax.dot_general(a, b, (((1,), (0,)), ((), ())), preferred_element_type=F32)


def mm_nt(a, b):
    return lax.dot_general(a, b, (((1,), (1,)), ((), ())), preferred_element_type=F32)


def wait_rows(ref, rows, sem):
    view = ref.at[pl.ds(0, rows)]
    pltpu.make_async_copy(view, view, sem).wait()


def kernel(
    fetch_s, list_s, count_s, rank_s, g_ref, dcol_ref,
    colour_ref, grad_ref,
    w_ref, u_ref, wsplit_ref, wcol_ref, crow_ref, mom_ref, dpad_ref,
    fold_ref, unfold_ref, hot_ref, pick_ref, hot_t_ref, rank_ref, lit_ref, dens_ref,
    send_s, send_a, recv_s, recv_a, all_x, send_d, recv_d, send_f, recv_f, send_c, recv_c,
    send_sem, recv_sem,
):
    cell = lax.axis_index("cell")
    own = lax.axis_index("own")
    own_y = own // 8
    own_z = own % 8
    holder = own_y == cell

    barrier = pltpu.get_barrier_semaphore()

    def greet(i, carry):
        pl.semaphore_signal(barrier, inc=1, device_id=(cell, (own + i) % OWN), device_id_type=MESH)
        return carry

    lax.fori_loop(1, OWN, greet, 0)
    for i in range(1, CELL):
        pl.semaphore_signal(barrier, inc=1, device_id=((cell + i) % CELL, own), device_id_type=MESH)

    lane1 = iota((1, GP), 1)
    lane8 = iota((8, GP), 1)
    row8 = iota((8, GP), 0)
    chan8 = (lane8 % 16) // 4

    live_n = count_s[0, 0]
    aux = jnp.zeros((1, GP), jnp.int32)
    for entry in range(LIST):
        slot = list_s[0, entry]
        peer = slot // CAP
        block = fetch_s[slot % CAP, peer] - peer * BLK
        live = (entry < live_n).astype(jnp.int32)
        aux = jnp.where(lane1 == L_PEER + entry, live * (peer + 1) - 1, aux)
        aux = jnp.where(lane1 == L_BLK + entry, block, aux)
    for c in range(CELL):
        aux = jnp.where(lane1 == L_RANK + c, rank_s[0, c], aux)
    aux = jnp.broadcast_to(aux.astype(F32), (8, GP))
    dpad_ref[...] = jnp.zeros((8, GP), F32)
    for k in range(3):
        dpad_ref[k : k + 1, 0:32] = dcol_ref[k]
    slanted = pltpu.roll(dpad_ref[...], 0, 1, stride=4, stride_axis=0)
    of_row = ((lane8 - L_DCOL) // 4 == row8) & (lane8 >= L_DCOL) & (row8 < 3)
    dcol_rows = jnp.zeros((8, GP), F32)
    for i in range(8):
        moved = jnp.where(of_row, pltpu.roll(slanted, L_DCOL - 4 * i, 1), 0.0)
        moved = jnp.broadcast_to(jnp.sum(moved, axis=0, keepdims=True), (8, GP))
        dcol_rows = jnp.where(row8 == i, moved, dcol_rows)
    for i in range(8):
        mine = (cell == i).astype(F32)
        send_a[8 * i : 8 * i + 8, 0, :] = aux + mine * dcol_rows

    mean_x, mean_y = g_ref[0], g_ref[1]
    inv_a, inv_c = jnp.exp(g_ref[2]), jnp.exp(g_ref[3])
    mid = jnp.exp(0.5 * (g_ref[2] + g_ref[3]))
    cross = g_ref[4] * mid
    opacity = jax.nn.sigmoid(g_ref[5])
    crow_ref[...] = jnp.zeros((32, GP), F32)
    for k in range(3):
        crow_ref[pl.ds(k, 8, stride=4), :] = g_ref[6 + k]
    crow = crow_ref[...]
    row32 = iota((32, GP), 0)
    before_of = (iota((2 * GP, GP), 0) % GP < iota((2 * GP, GP), 1)).astype(F32).astype(BF16)
    xs = [(4 * (row8 % 4) + r).astype(F32) + 0.5 for r in range(NPX)]
    ys = (2 * iota((8, 8, GP), 0) + iota((8, 8, GP), 1) // 4).astype(F32) + 0.5

    total = jnp.zeros((256, 64), F32)
    for b in range(BLK):
        of = lambda v: jnp.broadcast_to(v[b : b + 1, :], (8, GP))
        mx, my, ca, cc, cb, op = (of(v) for v in (mean_x, mean_y, inv_a, inv_c, cross, opacity))
        dy = ys - my[None]
        part_y = (-0.5 * cc)[None] * dy * dy
        slope = cb[None] * dy
        covs = []
        for r in range(NPX):
            dx = xs[r] - mx
            covs.append(op[None] * jnp.exp(part_y - (0.5 * ca * dx * dx)[None] - dx[None] * slope))
        cov = jnp.stack(covs, axis=0).reshape(256, GP)
        keep_log = jnp.log(1.0 - cov)
        log_hi, log_lo = split(keep_log)
        before = mm(jnp.concatenate([log_hi, log_lo], axis=1), before_of)
        weight = jnp.exp(before) * cov
        w_hi, w_lo = split(weight)
        colour_b = jnp.where(row32 // 4 == b, crow, 0.0)
        ones_b = jnp.where(row32 == 4 * b + 3, 1.0, 0.0).astype(BF16)
        c_hi, c_lo = split(colour_b)
        none = jnp.zeros((32, GP), BF16)
        top = jnp.concatenate([c_hi, ones_b], axis=1)
        low = jnp.concatenate([c_lo, none], axis=1)
        wcol_ref[b] = jnp.concatenate([top, low, top, jnp.concatenate([none, none], axis=1)], axis=0)
        both = jnp.concatenate([top, low], axis=0)
        total += mm_nt(jnp.concatenate([w_hi, log_hi], axis=1), both)
        total += mm_nt(jnp.concatenate([w_lo, log_lo], axis=1), both)
        w_ref[b] = weight
        u_ref[b] = cov * jnp.exp(-keep_log)
        wsplit_ref[b] = jnp.concatenate([w_hi, w_lo], axis=1)
    total = jnp.concatenate([total, jnp.zeros((256, 64), F32)], axis=1)
    total = jnp.where(iota((256, GP), 1) < 32, total + pltpu.roll(total, 96, 1), 0.0)
    rows = total[0:64]
    for r in range(1, NPX):
        rows += pltpu.roll(total[64 * r : 64 * r + 64], 32 * r, 1)
    send_s[:, 0, :] = rows

    pl.semaphore_wait(barrier, OWN - 1 + CELL - 1)

    def spread_rows(source, target, slot):
        def one(i, carry):
            peer = (own + i) % OWN
            pltpu.make_async_remote_copy(
                source.at[peer], target.at[own], send_sem.at[slot], recv_sem.at[slot],
                device_id=(cell, peer), device_id_type=MESH,
            ).start()
            return carry

        lax.fori_loop(1, OWN, one, 0)
        target[pl.ds(own, 1)] = source[pl.ds(own, 1)]

    spread_rows(send_a, recv_a, 0)
    spread_rows(send_s, recv_s, 1)

    for a in range(8):
        lane_in = iota((GP, GP), 0)
        lane_out = iota((GP, GP), 1)
        same = (lane_out // 16 == a) & (lane_out % 4 == lane_in // 32)
        to_own = same & ((lane_out % 16) // 4 == lane_in % 4)
        to_all = same & (lane_in % 4 == 3)
        piece = jnp.concatenate([to_own.astype(F32), to_all.astype(F32)], axis=1).astype(BF16)
        fold_ref[256 * a : 256 * a + 128, :] = piece
        fold_ref[256 * a + 128 : 256 * a + 256, :] = piece
        back = (lane_in // 16 == a) & (lane_in % 4 == lane_out // 32) & ((lane_in % 16) // 4 == lane_out % 4)
        back = back.astype(F32).astype(BF16)
        unfold_ref[0:128, 128 * a : 128 * a + 128] = back
        unfold_ref[128:256, 128 * a : 128 * a + 128] = back

    wait_rows(recv_a, OWN - 1, recv_sem.at[0])
    lane8f = lane8.astype(F32)
    block8f = ((lane8 // 4) % 8).astype(F32)
    dense_d = jnp.zeros((8, GP), F32)
    dense_r = jnp.zeros((8, GP), F32)
    for a in range(8):
        tile_rows = recv_a[8 * a : 8 * a + 8, 0, :]
        here = lane8 // 16 == a
        dense_d = jnp.where(here, pltpu.roll(tile_rows, (16 * a - L_DCOL) % GP, 1), dense_d)
        dense_r = jnp.where(here, pltpu.roll(tile_rows, (16 * a - L_RANK) % GP, 1), dense_r)
        hots, picks = [], []
        for entry in range(LIST):
            peer = jnp.broadcast_to(tile_rows[:, L_PEER + entry : L_PEER + entry + 1], (8, GP))
            block = jnp.broadcast_to(tile_rows[:, L_BLK + entry : L_BLK + entry + 1], (8, GP))
            hots.append(jnp.where(peer == lane8f, 1.0, 0.0))
            picks.append(jnp.where(block == block8f, 1.0, 0.0))
        hot_ref[96 * a : 96 * a + 96, :] = jnp.concatenate(hots, axis=0)
        pick_ref[96 * a : 96 * a + 96, :] = jnp.concatenate(picks, axis=0).astype(BF16)
    dense_d = jnp.where(chan8 < 3, dense_d, 0.0)

    @pl.when(holder)
    def _():
        send_d[...] = dense_d
        recv_d[...] = dense_d
        for i in range(1, CELL):
            pltpu.make_async_remote_copy(
                send_d, recv_d, send_sem.at[2], recv_sem.at[2],
                device_id=((cell + i) % CELL, own), device_id_type=MESH,
            ).start()

    one_rank = jnp.concatenate([jnp.where(lane8 % 16 == c, dense_r, 0.0) for c in range(CELL)], axis=0)
    group = (iota((GP, GP), 0) // 16 == iota((GP, GP), 1) // 16).astype(F32).astype(BF16)
    rank_ref[...] = mm(one_rank.astype(BF16), group).reshape(8, 8, GP)

    wait_rows(recv_s, OWN - 1, recv_sem.at[1])
    s_hi, s_lo = split(recv_s[:, 0, :])
    taken = mm(hot_ref[...].astype(BF16)[:, 0:64], jnp.concatenate([s_hi, s_lo], axis=1)).astype(BF16)
    pick = pick_ref[...]
    taken = taken * jnp.concatenate([pick, pick], axis=1)
    taken = jnp.concatenate([taken[96 * a : 96 * a + 96] for a in range(8)], axis=1)
    folded = mm(taken, fold_ref[...])
    entry_c = folded[:, 0:128].reshape(LIST, 8, GP)
    entry_t = folded[:, 128:256].reshape(LIST, 8, GP)
    ahead = jnp.zeros((8, GP), F32)
    part = jnp.zeros((8, GP), F32)
    for entry in range(LIST):
        seen = jnp.exp(ahead)
        dens_ref[entry] = seen
        part += seen * entry_c[entry]
        ahead += entry_t[entry]
    all_x[cell] = jnp.where(chan8 < 3, part, ahead)
    for i in range(1, CELL):
        pltpu.make_async_remote_copy(
            all_x.at[cell], all_x.at[cell], send_sem.at[3], recv_sem.at[3],
            device_id=((cell + i) % CELL, own), device_id_type=MESH,
        ).start()

    hot_t_ref[...] = hot_ref[...].T[0:64].astype(BF16)
    ranks = [rank_ref[c] for c in range(CELL)]

    @pl.when(jnp.logical_not(holder))
    def _():
        pltpu.make_async_copy(recv_d, recv_d, recv_sem.at[2]).wait()

    wait_rows(all_x, CELL - 1, recv_sem.at[3])

    dense_d = recv_d[...]
    parts = [all_x[c] for c in range(CELL)]
    logs, dots = [], []
    for c in range(CELL):
        last = jnp.where(chan8 == 3, parts[c], 0.0)
        logs.append(last + pltpu.roll(last, 124, 1) + pltpu.roll(last, 120, 1) + pltpu.roll(last, 116, 1))
        lossy = parts[c] * dense_d
        dots.append(pltpu.roll(lossy, 4, 1) + pltpu.roll(lossy, 8, 1) + pltpu.roll(lossy, 12, 1))
    colour = jnp.zeros((8, GP), F32)
    behind = jnp.zeros((8, GP), F32)
    my_rank = rank_ref[cell]
    for c in range(CELL):
        shade = jnp.zeros((8, GP), F32)
        for other in range(CELL):
            if other != c:
                shade += jnp.where(ranks[other] < ranks[c], logs[other], 0.0)
        lit = jnp.exp(shade)
        lit_ref[c] = lit
        colour += lit * parts[c]
        behind += jnp.where(ranks[c] > my_rank, lit * dots[c], 0.0)
    d_part = dense_d * lit_ref[cell]
    grad_rows = [None] * LIST
    for entry in reversed(range(LIST)):
        d_c = dens_ref[entry] * d_part
        grad_rows[entry] = jnp.where(chan8 < 3, d_c, behind)
        lossy = d_c * entry_c[entry]
        behind = behind + (pltpu.roll(lossy, 4, 1) + pltpu.roll(lossy, 8, 1) + pltpu.roll(lossy, 12, 1))
    g_hi, g_lo = split(jnp.concatenate(grad_rows, axis=0))
    wide = mm(jnp.concatenate([g_hi, g_lo], axis=1), unfold_ref[...])
    wide = jnp.concatenate([wide[:, 128 * a : 128 * a + 128] for a in range(8)], axis=0)
    wide_hi, wide_lo = split(wide)
    wide = jnp.concatenate([wide_hi * pick, wide_lo * pick], axis=1)
    back = mm(hot_t_ref[...], wide)
    send_f[:, 0, :] = back[:, 0:128] + back[:, 128:256]
    spread_rows(send_f, recv_f, 4)

    for a in range(8):
        send_c[8 * a : 8 * a + 8, 0, :] = pltpu.roll(colour, (GP - 16 * a) % GP, 1)

    @pl.when(holder)
    def _():
        def one(i, carry):
            peer = (own + i) % OWN
            pltpu.make_async_remote_copy(
                send_c.at[peer], recv_c.at[own_z], send_sem.at[5], recv_sem.at[5],
                device_id=(cell, peer), device_id_type=MESH,
            ).start()
            return carry

        lax.fori_loop(1, OWN, one, 0)
        recv_c[pl.ds(own_z, 1)] = send_c[pl.ds(own, 1)]

    after_of = (iota((2 * GP, GP), 0) % GP > iota((2 * GP, GP), 1)).astype(F32).astype(BF16)
    wait_rows(recv_f, OWN - 1, recv_sem.at[4])
    cot = recv_f[:, 0, :]
    cot_hi = cot.astype(BF16).astype(F32)
    cot_lo = cot - cot_hi
    lane64 = iota((64, GP), 1)
    left = []
    for r in range(NPX):
        one = pltpu.roll(cot_hi, (GP - 32 * r) % GP, 1)
        two = pltpu.roll(cot_hi, (GP + 32 - 32 * r) % GP, 1)
        three = pltpu.roll(cot_lo, (GP + 64 - 32 * r) % GP, 1)
        left.append(jnp.where(lane64 < 32, one, jnp.where(lane64 < 64, two, jnp.where(lane64 < 96, three, 0.0))))
    left = jnp.concatenate(left, axis=0).astype(BF16)
    turned = jnp.concatenate([cot, jnp.zeros((64, GP), F32)], axis=0).T
    turned = jnp.concatenate(
        [
            turned[0:32] + pltpu.roll(turned[32:64], 64, 1),
            turned[64:96] + pltpu.roll(turned[96:128], 64, 1),
        ],
        axis=1,
    )
    turned = jnp.concatenate(split(turned), axis=0)
    d_colour = jnp.zeros((32, GP), F32)
    for b in range(BLK):
        of = lambda v: jnp.broadcast_to(v[b : b + 1, :], (8, GP))
        mx, my = of(mean_x), of(mean_y)
        pair = mm(left, wcol_ref[b])
        d_before = pair[:, 0:128] * w_ref[b]
        after = mm(jnp.concatenate(split(d_before), axis=1), after_of)
        flow = (d_before - (pair[:, 128:256] + after) * u_ref[b]).reshape(NPX, 8, 8, GP)
        dy = ys - my[None]
        m0 = mxs = mxx = mys = mxy = myy = jnp.zeros((8, GP), F32)
        for r in range(NPX):
            dx = xs[r] - mx
            q = flow[r]
            qy = q * dy
            s0, s1 = jnp.sum(q, axis=0), jnp.sum(qy, axis=0)
            m0 += s0
            mxs += s0 * dx
            mxx += s0 * dx * dx
            mys += s1
            mxy += s1 * dx
            myy += jnp.sum(qy * dy, axis=0)
        for i, m in enumerate((m0, mxs, mxx, mys, mxy, myy)):
            mom_ref[i, b : b + 1, :] = jnp.sum(m, axis=0, keepdims=True)
        grown = mm(turned, wsplit_ref[b])
        grown = grown[0:32, 0:128] + grown[0:32, 128:256] + grown[32:64, 0:128]
        d_colour = jnp.where(row32 // 4 == b, grown, d_colour)
    m0, mxs, mxx, mys, mxy, myy = (mom_ref[i] for i in range(6))
    grad_ref[0] = inv_a * mxs + cross * mys
    grad_ref[1] = inv_c * mys + cross * mxs
    grad_ref[2] = -0.5 * (inv_a * mxx + cross * mxy)
    grad_ref[3] = -0.5 * (inv_c * myy + cross * mxy)
    grad_ref[4] = -mid * mxy
    grad_ref[5] = (1.0 - opacity) * m0
    crow_ref[...] = d_colour
    for k in range(3):
        grad_ref[6 + k] = crow_ref[pl.ds(k, 8, stride=4), :]

    @pl.when(holder)
    def _():
        wait_rows(recv_c, 7, recv_sem.at[5])

    @pl.when(jnp.logical_not(holder))
    def _():
        wait_rows(recv_c, 8, recv_sem.at[5])

    tile = pltpu.roll(recv_c[:, 0, :], 0, 1, stride=4, stride_axis=0)
    for k in range(3):
        moved = pltpu.roll(tile, (GP - 4 * k) % GP, 1)
        moved = jnp.where(lane8 // 4 == row8, moved, 0.0)
        colour_ref[k] = jnp.sum(moved, axis=0, keepdims=True)[:, 0:32]

    for source, slot in ((send_a, 0), (send_s, 1), (send_f, 4)):
        wait_rows(source, OWN - 1, send_sem.at[slot])
    wait_rows(all_x, CELL - 1, send_sem.at[3])

    @pl.when(holder)
    def _():
        wait_rows(send_c, OWN - 1, send_sem.at[5])
        wait_rows(all_x, CELL - 1, send_sem.at[2])


def body(gaussians, fetch_ids, tile_lists, counts, cell_rank, d_colour):
    fetch = jnp.transpose(fetch_ids, (0, 1, 3, 2)).reshape(CAP, OWN)
    lists = tile_lists.reshape(1, LIST)
    params = jnp.transpose(gaussians, (1, 0, 2))
    d_rows = jnp.transpose(d_colour, (1, 0, 2))
    smem = pl.BlockSpec(memory_space=pltpu.SMEM)
    vmem = pl.BlockSpec(memory_space=pltpu.VMEM)
    row = lambda n: pltpu.VMEM((n, 1, GP), F32)
    colour, grads = pl.pallas_call(
        kernel,
        out_shape=(
            jax.ShapeDtypeStruct((3, 1, 32), F32),
            jax.ShapeDtypeStruct((9, BLK, GP), F32),
        ),
        in_specs=[smem, smem, smem, smem, vmem, vmem],
        out_specs=(vmem, vmem),
        scratch_shapes=[
            pltpu.VMEM((BLK, 256, GP), F32),
            pltpu.VMEM((BLK, 256, GP), F32),
            pltpu.VMEM((BLK, 256, 256), BF16),
            pltpu.VMEM((BLK, GP, 256), BF16),
            pltpu.VMEM((32, GP), F32),
            pltpu.VMEM((6, 8, GP), F32),
            pltpu.VMEM((8, GP), F32),
            pltpu.VMEM((2048, 256), BF16),
            pltpu.VMEM((256, 1024), BF16),
            pltpu.VMEM((768, GP), F32),
            pltpu.VMEM((768, GP), BF16),
            pltpu.VMEM((64, 768), BF16),
            pltpu.VMEM((8, 8, GP), F32),
            pltpu.VMEM((8, 8, GP), F32),
            pltpu.VMEM((LIST, 8, GP), F32),
            row(64), row(64), row(64), row(64),
            pltpu.VMEM((8, 8, GP), F32),
            pltpu.VMEM((8, GP), F32),
            pltpu.VMEM((8, GP), F32),
            row(64), row(64), row(64), row(8),
            pltpu.SemaphoreType.DMA((6,)),
            pltpu.SemaphoreType.DMA((6,)),
        ],
        compiler_params=pltpu.CompilerParams(
            collective_id=0, has_side_effects=True, vmem_limit_bytes=32 << 20
        ),
    )(fetch, lists, counts, cell_rank, params, d_rows)
    return jnp.transpose(colour, (1, 0, 2)), jnp.transpose(grads, (1, 0, 2))


def solution(mesh):
    in_specs = (
        P(("cell", "own"), None, None),
        P("cell", "own", None, None),
        P("cell", "own", None),
        P("cell", "own"),
        P("own", None),
        P("own", None, "cell"),
    )
    out_specs = (P("own", None, "cell"), P(("cell", "own"), None, None))
    return jax.shard_map(body, mesh=mesh, in_specs=in_specs, out_specs=out_specs, check_vma=False)
```

time: 155 us -> 45.5 us (0.29)
  the two profiles are of different devices: /device:TPU:16 before, /device:TPU:1 now
where the time goes in v1:
time: 45.5 us; the launch traced here: 45.3 us
  Pallas kernels  41.4 us (91%)
  local copies, waits for them, and re-layouts  2.64 us (6%)
  between operations  1.32 us (3%)
    pallas_call x1, Pallas kernels, body(): pl.pallas_call(kernel, out_shape=(jax.ShapeDtypeStruct((3, 1, 32), F32),...  41.4 us
    unnamed x12, local copies, waits for them, and re-layouts  2.64 us

profile of v1, /device:TPU:1, one launch (start us, length us, event | category | flops | bytes accessed | tf_op | source)
XLA Modules:
  0.0 45.3 jit_solution(1450860339688218974)
XLA Ops:
  1.3 0.0 copy-start.3
  1.3 0.0 copy-start.4
  1.3 0.0 copy-start.1
  1.3 0.0 copy-start.2
  1.3 0.6 %copy-done.3 = s32[1,1,12]{2,1,0:T(1,128)S(1)} copy-done((s32[1,1,12]{2,1,0:T(1,128)S(1)}, s32[1,1,12]{2,1,0:T(1,128)}, u32[]{:S(2)}) %copy-start.3) | copy-done | bytes 72
  1.9 0.0 copy-done.4
  1.9 0.0 copy-done.1
  2.0 0.0 copy-done.2
  2.0 0.0 copy-start
  2.0 0.8 %copy-done = f32[8,9,128]{2,0,1:T(8,128)S(1)} copy-done((f32[8,9,128]{2,0,1:T(8,128)S(1)}, f32[8,9,128]{2,0,1:T(8,128)}, u32[]{:S(2)}) %copy-start) | copy-done | bytes 36888
  2.8 41.4 %shard_map.77 = (f32[3,1,32]{2,1,0:T(1,128)S(1)}, f32[9,8,128]{2,1,0:T(8,128)S(1)}) custom-call(s32[4,64]{1,0:T(4,128)S(1)} %bitcast.10, s32[1,12]{1,0:T(1,128)S(1)} %bitcast.13, s32[1,1]{1,0:T(1,128)S(6)} %copy.10.count_s, s32[1,8]{1,0:T(1,128)S(1)} %copy-done.4, f32[9,8,128]{2,1,0:T(8,128)S(1)} %bitcast.8, f32[3,1,32]{2,1,0:T(1,128)S(1)} %bitcast.12), custom_call_target="tpu_custom_call" | custom-call | tf_op jit(solution)/shard_map/pallas_call | solution.py:390
  44.1 0.6 %copy.11 = f32[1,3,32]{2,0,1:T(1,128)} copy(f32[1,3,32]{2,0,1:T(1,128)S(1)} %bitcast.11) | data formatting | bytes 768
  44.7 0.6 %copy.12 = f32[8,9,128]{2,0,1:T(8,128)} copy(f32[8,9,128]{2,0,1:T(8,128)S(1)} %bitcast.9) | data formatting | bytes 73728
Async XLA Ops:
  1.3 0.7 %copy-start.3 = (s32[1,1,12]{2,1,0:T(1,128)S(1)}, s32[1,1,12]{2,1,0:T(1,128)}, u32[]{:S(2)}) copy-start(s32[1,1,12]{2,1,0:T(1,128)} %param.8) | copy-start | bytes 148
  1.3 0.7 %copy-start.4 = (s32[1,8]{1,0:T(1,128)S(1)}, s32[1,8]{1,0:T(1,128)}, u32[]{:S(2)}) copy-start(s32[1,8]{1,0:T(1,128)} %rank_s.1) | copy-start | bytes 100
  1.3 0.7 %copy-start.1 = (s32[1,1,64,4]{2,3,1,0:T(4,128)S(1)}, s32[1,1,64,4]{2,3,1,0:T(4,128)}, u32[]{:S(2)}) copy-start(s32[1,1,64,4]{2,3,1,0:T(4,128)} %param.7) | copy-start | bytes 3076
  1.3 0.7 %copy-start.2 = (f32[1,3,32]{2,0,1:T(1,128)S(1)}, f32[1,3,32]{2,0,1:T(1,128)}, u32[]{:S(2)}) copy-start(f32[1,3,32]{2,0,1:T(1,128)} %param.11) | copy-start | bytes 1156
  2.0 0.8 %copy-start = (f32[8,9,128]{2,0,1:T(8,128)S(1)}, f32[8,9,128]{2,0,1:T(8,128)}, u32[]{:S(2)}) copy-start(f32[8,9,128]{2,0,1:T(8,128)} %param.6) | copy-start | bytes 110596

commit v2 on v1

--- a/solution.py
+++ b/solution.py
@@ -13,6 +13,7 @@
 CAP = 4
 OWN = 64
 CELL = 8
+CELL_ORDER = (4, 3, 5, 2, 6, 1, 7)
 BLK = 8
 GP = 128
 NPX = 4
@@ -42,34 +43,53 @@
 
 
 def kernel(
-    fetch_s, list_s, count_s, rank_s, g_ref, dcol_ref,
+    fetch_h, list_h, count_h, rank_h, g_h, dcol_h,
     colour_ref, grad_ref,
+    fetch_s, list_s, count_s, rank_s, g_ref, dcol_ref, in_sem,
     w_ref, u_ref, wsplit_ref, wcol_ref, crow_ref, mom_ref, dpad_ref,
     fold_ref, unfold_ref, hot_ref, pick_ref, hot_t_ref, rank_ref, lit_ref, dens_ref,
-    send_s, send_a, recv_s, recv_a, all_x, send_d, recv_d, send_f, recv_f, send_c, recv_c,
+    send_b, recv_b, all_x, send_d, recv_d, send_f, recv_f, send_c, recv_c,
     send_sem, recv_sem,
 ):
     cell = lax.axis_index("cell")
     own = lax.axis_index("own")
-    own_y = own // 8
-    own_z = own % 8
+    own_y = lax.div(own, 8)
+    own_z = lax.rem(own, 8)
     holder = own_y == cell
 
+    def far_first(visit):
+        def pair(k, carry):
+            visit(lax.rem(own + 36 + k, OWN))
+            visit(lax.rem(own + 35 - k, OWN))
+            return carry
+
+        def near(k, carry):
+            visit(lax.rem(own + 7 - k, OWN))
+            return carry
+
+        lax.fori_loop(0, 28, pair, 0)
+        lax.fori_loop(0, 7, near, 0)
+
     barrier = pltpu.get_barrier_semaphore()
-
-    def greet(i, carry):
-        pl.semaphore_signal(barrier, inc=1, device_id=(cell, (own + i) % OWN), device_id_type=MESH)
-        return carry
-
-    lax.fori_loop(1, OWN, greet, 0)
-    for i in range(1, CELL):
-        pl.semaphore_signal(barrier, inc=1, device_id=((cell + i) % CELL, own), device_id_type=MESH)
+    far_first(lambda peer: pl.semaphore_signal(barrier, inc=1, device_id=(cell, peer), device_id_type=MESH))
+    for i in CELL_ORDER:
+        pl.semaphore_signal(barrier, inc=1, device_id=(lax.rem(cell + i, CELL), own), device_id_type=MESH)
+    loads = [
+        pltpu.make_async_copy(source, target, in_sem.at[i])
+        for i, (source, target) in enumerate(
+            [(g_h, g_ref), (fetch_h, fetch_s), (list_h, list_s), (count_h, count_s), (rank_h, rank_s), (dcol_h, dcol_ref)]
+        )
+    ]
+    for load in loads:
+        load.start()
 
     lane1 = iota((1, GP), 1)
     lane8 = iota((8, GP), 1)
     row8 = iota((8, GP), 0)
     chan8 = (lane8 % 16) // 4
 
+    for load in loads:
+        load.wait()
     live_n = count_s[0, 0]
     aux = jnp.zeros((1, GP), jnp.int32)
     for entry in range(LIST):
@@ -94,7 +114,7 @@
         dcol_rows = jnp.where(row8 == i, moved, dcol_rows)
     for i in range(8):
         mine = (cell == i).astype(F32)
-        send_a[8 * i : 8 * i + 8, 0, :] = aux + mine * dcol_rows
+        send_b[pl.ds(16 * i + 1, 8, stride=2), :] = aux + mine * dcol_rows
 
     mean_x, mean_y = g_ref[0], g_ref[1]
     inv_a, inv_c = jnp.exp(g_ref[2]), jnp.exp(g_ref[3])
@@ -145,24 +165,22 @@
     rows = total[0:64]
     for r in range(1, NPX):
         rows += pltpu.roll(total[64 * r : 64 * r + 64], 32 * r, 1)
-    send_s[:, 0, :] = rows
+    send_b[pl.ds(0, 64, stride=2), :] = rows
 
     pl.semaphore_wait(barrier, OWN - 1 + CELL - 1)
 
-    def spread_rows(source, target, slot):
-        def one(i, carry):
-            peer = (own + i) % OWN
+    def spread_rows(source, target, rows, slot):
+        def one(peer):
             pltpu.make_async_remote_copy(
-                source.at[peer], target.at[own], send_sem.at[slot], recv_sem.at[slot],
-                device_id=(cell, peer), device_id_type=MESH,
+                source.at[pl.ds(rows * peer, rows)], target.at[pl.ds(rows * own, rows)],
+                send_sem.at[slot], recv_sem.at[slot], device_id=(cell, peer), device_id_type=MESH,
             ).start()
-            return carry
-
-        lax.fori_loop(1, OWN, one, 0)
-        target[pl.ds(own, 1)] = source[pl.ds(own, 1)]
-
-    spread_rows(send_a, recv_a, 0)
-    spread_rows(send_s, recv_s, 1)
+
+        far_first(one)
+        for i in range(rows):
+            target[pl.ds(rows * own + i, 1), :] = source[pl.ds(rows * own + i, 1), :]
+
+    spread_rows(send_b, recv_b, 2, 0)
 
     for a in range(8):
         lane_in = iota((GP, GP), 0)
@@ -178,44 +196,47 @@
         unfold_ref[0:128, 128 * a : 128 * a + 128] = back
         unfold_ref[128:256, 128 * a : 128 * a + 128] = back
 
-    wait_rows(recv_a, OWN - 1, recv_sem.at[0])
+    choose_in = iota((GP, 256), 0)
+    choose_out = iota((GP, 256), 1)
+    choose = (choose_in < 16) & (choose_out < 128) | (choose_in >= 32) & (choose_in < 48) & (choose_out >= 128)
+    choose = choose.astype(F32).astype(BF16)
+    wait_rows(recv_b, 2 * (OWN - 1), recv_sem.at[0])
     lane8f = lane8.astype(F32)
     block8f = ((lane8 // 4) % 8).astype(F32)
     dense_d = jnp.zeros((8, GP), F32)
     dense_r = jnp.zeros((8, GP), F32)
+    lone = []
     for a in range(8):
-        tile_rows = recv_a[8 * a : 8 * a + 8, 0, :]
+        tile_rows = recv_b[pl.ds(16 * a + 1, 8, stride=2), :]
         here = lane8 // 16 == a
         dense_d = jnp.where(here, pltpu.roll(tile_rows, (16 * a - L_DCOL) % GP, 1), dense_d)
         dense_r = jnp.where(here, pltpu.roll(tile_rows, (16 * a - L_RANK) % GP, 1), dense_r)
-        hots, picks = [], []
         for entry in range(LIST):
-            peer = jnp.broadcast_to(tile_rows[:, L_PEER + entry : L_PEER + entry + 1], (8, GP))
-            block = jnp.broadcast_to(tile_rows[:, L_BLK + entry : L_BLK + entry + 1], (8, GP))
-            hots.append(jnp.where(peer == lane8f, 1.0, 0.0))
-            picks.append(jnp.where(block == block8f, 1.0, 0.0))
-        hot_ref[96 * a : 96 * a + 96, :] = jnp.concatenate(hots, axis=0)
-        pick_ref[96 * a : 96 * a + 96, :] = jnp.concatenate(picks, axis=0).astype(BF16)
+            mine = (lane8 == L_PEER + entry) | (lane8 == L_BLK + entry)
+            lone.append(jnp.where(mine, tile_rows, 0.0))
+    named = mm(jnp.concatenate(lone, axis=0).astype(BF16), choose).reshape(96, 8, 256)
+    hot = jnp.where(named[:, :, 0:128] == lane8f[None], 1.0, 0.0).reshape(768, GP)
+    pick = jnp.where(named[:, :, 128:256] == block8f[None], 1.0, 0.0).reshape(768, GP).astype(BF16)
+    hot_ref[...] = hot
+    pick_ref[...] = pick
     dense_d = jnp.where(chan8 < 3, dense_d, 0.0)
 
     @pl.when(holder)
     def _():
         send_d[...] = dense_d
         recv_d[...] = dense_d
-        for i in range(1, CELL):
+        for i in CELL_ORDER:
             pltpu.make_async_remote_copy(
                 send_d, recv_d, send_sem.at[2], recv_sem.at[2],
-                device_id=((cell + i) % CELL, own), device_id_type=MESH,
+                device_id=(lax.rem(cell + i, CELL), own), device_id_type=MESH,
             ).start()
 
     one_rank = jnp.concatenate([jnp.where(lane8 % 16 == c, dense_r, 0.0) for c in range(CELL)], axis=0)
     group = (iota((GP, GP), 0) // 16 == iota((GP, GP), 1) // 16).astype(F32).astype(BF16)
     rank_ref[...] = mm(one_rank.astype(BF16), group).reshape(8, 8, GP)
 
-    wait_rows(recv_s, OWN - 1, recv_sem.at[1])
-    s_hi, s_lo = split(recv_s[:, 0, :])
-    taken = mm(hot_ref[...].astype(BF16)[:, 0:64], jnp.concatenate([s_hi, s_lo], axis=1)).astype(BF16)
-    pick = pick_ref[...]
+    s_hi, s_lo = split(recv_b[pl.ds(0, 64, stride=2), :])
+    taken = mm(hot.astype(BF16)[:, 0:64], jnp.concatenate([s_hi, s_lo], axis=1)).astype(BF16)
     taken = taken * jnp.concatenate([pick, pick], axis=1)
     taken = jnp.concatenate([taken[96 * a : 96 * a + 96] for a in range(8)], axis=1)
     folded = mm(taken, fold_ref[...])
@@ -229,10 +250,10 @@
         part += seen * entry_c[entry]
         ahead += entry_t[entry]
     all_x[cell] = jnp.where(chan8 < 3, part, ahead)
-    for i in range(1, CELL):
+    for i in CELL_ORDER:
         pltpu.make_async_remote_copy(
             all_x.at[cell], all_x.at[cell], send_sem.at[3], recv_sem.at[3],
-            device_id=((cell + i) % CELL, own), device_id_type=MESH,
+            device_id=(lax.rem(cell + i, CELL), own), device_id_type=MESH,
         ).start()
 
     hot_t_ref[...] = hot_ref[...].T[0:64].astype(BF16)
@@ -271,34 +292,32 @@
         grad_rows[entry] = jnp.where(chan8 < 3, d_c, behind)
         lossy = d_c * entry_c[entry]
         behind = behind + (pltpu.roll(lossy, 4, 1) + pltpu.roll(lossy, 8, 1) + pltpu.roll(lossy, 12, 1))
+    pick = pick_ref[...]
     g_hi, g_lo = split(jnp.concatenate(grad_rows, axis=0))
     wide = mm(jnp.concatenate([g_hi, g_lo], axis=1), unfold_ref[...])
     wide = jnp.concatenate([wide[:, 128 * a : 128 * a + 128] for a in range(8)], axis=0)
     wide_hi, wide_lo = split(wide)
     wide = jnp.concatenate([wide_hi * pick, wide_lo * pick], axis=1)
     back = mm(hot_t_ref[...], wide)
-    send_f[:, 0, :] = back[:, 0:128] + back[:, 128:256]
-    spread_rows(send_f, recv_f, 4)
+    send_f[...] = back[:, 0:128] + back[:, 128:256]
+    spread_rows(send_f, recv_f, 1, 4)
 
     for a in range(8):
-        send_c[8 * a : 8 * a + 8, 0, :] = pltpu.roll(colour, (GP - 16 * a) % GP, 1)
+        send_c[8 * a : 8 * a + 8, :] = pltpu.roll(colour, (GP - 16 * a) % GP, 1)
 
     @pl.when(holder)
     def _():
-        def one(i, carry):
-            peer = (own + i) % OWN
-            pltpu.make_async_remote_copy(
-                send_c.at[peer], recv_c.at[own_z], send_sem.at[5], recv_sem.at[5],
+        far_first(
+            lambda peer: pltpu.make_async_remote_copy(
+                send_c.at[pl.ds(peer, 1)], recv_c.at[pl.ds(own_z, 1)], send_sem.at[5], recv_sem.at[5],
                 device_id=(cell, peer), device_id_type=MESH,
             ).start()
-            return carry
-
-        lax.fori_loop(1, OWN, one, 0)
-        recv_c[pl.ds(own_z, 1)] = send_c[pl.ds(own, 1)]
+        )
+        recv_c[pl.ds(own_z, 1), :] = send_c[pl.ds(own, 1), :]
 
     after_of = (iota((2 * GP, GP), 0) % GP > iota((2 * GP, GP), 1)).astype(F32).astype(BF16)
     wait_rows(recv_f, OWN - 1, recv_sem.at[4])
-    cot = recv_f[:, 0, :]
+    cot = recv_f[...]
     cot_hi = cot.astype(BF16).astype(F32)
     cot_lo = cot - cot_hi
     lane64 = iota((64, GP), 1)
@@ -363,39 +382,69 @@
     def _():
         wait_rows(recv_c, 8, recv_sem.at[5])
 
-    tile = pltpu.roll(recv_c[:, 0, :], 0, 1, stride=4, stride_axis=0)
+    tile = pltpu.roll(recv_c[...], 0, 1, stride=4, stride_axis=0)
     for k in range(3):
         moved = pltpu.roll(tile, (GP - 4 * k) % GP, 1)
         moved = jnp.where(lane8 // 4 == row8, moved, 0.0)
         colour_ref[k] = jnp.sum(moved, axis=0, keepdims=True)[:, 0:32]
 
-    for source, slot in ((send_a, 0), (send_s, 1), (send_f, 4)):
-        wait_rows(source, OWN - 1, send_sem.at[slot])
+    wait_rows(send_b, 2 * (OWN - 1), send_sem.at[0])
+    wait_rows(send_f, OWN - 1, send_sem.at[4])
     wait_rows(all_x, CELL - 1, send_sem.at[3])
 
     @pl.when(holder)
     def _():
         wait_rows(send_c, OWN - 1, send_sem.at[5])
         wait_rows(all_x, CELL - 1, send_sem.at[2])
+
+
+def put(colour_ref, grad_ref, colour_out, grad_out, sem):
+    one = pltpu.make_async_copy(colour_ref, colour_out, sem.at[0])
+    two = pltpu.make_async_copy(grad_ref, grad_out, sem.at[1])
+    two.start()
+    one.start()
+    two.wait()
+    one.wait()
+
+
+def finish(colour, grads):
+    vmem = pl.BlockSpec(memory_space=pltpu.VMEM)
+    hbm = pl.BlockSpec(memory_space=pltpu.HBM)
+    return pl.pallas_call(
+        put,
+        out_shape=(jax.ShapeDtypeStruct(colour.shape, F32), jax.ShapeDtypeStruct(grads.shape, F32)),
+        in_specs=[vmem, vmem],
+        out_specs=(hbm, hbm),
+        scratch_shapes=[pltpu.SemaphoreType.DMA((2,))],
+        compiler_params=pltpu.CompilerParams(vmem_limit_bytes=1 << 20),
+    )(colour, grads)
 
 
 def body(gaussians, fetch_ids, tile_lists, counts, cell_rank, d_colour):
     fetch = jnp.transpose(fetch_ids, (0, 1, 3, 2)).reshape(CAP, OWN)
     lists = tile_lists.reshape(1, LIST)
+    hb = lambda v: pltpu.with_memory_space_constraint(v, pltpu.HBM)
     params = jnp.transpose(gaussians, (1, 0, 2))
     d_rows = jnp.transpose(d_colour, (1, 0, 2))
-    smem = pl.BlockSpec(memory_space=pltpu.SMEM)
+    hbm = pl.BlockSpec(memory_space=pltpu.HBM)
     vmem = pl.BlockSpec(memory_space=pltpu.VMEM)
-    row = lambda n: pltpu.VMEM((n, 1, GP), F32)
+    row = lambda n: pltpu.VMEM((n, GP), F32)
     colour, grads = pl.pallas_call(
         kernel,
         out_shape=(
             jax.ShapeDtypeStruct((3, 1, 32), F32),
             jax.ShapeDtypeStruct((9, BLK, GP), F32),
         ),
-        in_specs=[smem, smem, smem, smem, vmem, vmem],
+        in_specs=[hbm] * 6,
         out_specs=(vmem, vmem),
         scratch_shapes=[
+            pltpu.SMEM((CAP, OWN), jnp.int32),
+            pltpu.SMEM((1, LIST), jnp.int32),
+            pltpu.SMEM((1, 1), jnp.int32),
+            pltpu.SMEM((1, CELL), jnp.int32),
+            pltpu.VMEM((9, BLK, GP), F32),
+            pltpu.VMEM((3, 1, 32), F32),
+            pltpu.SemaphoreType.DMA((6,)),
             pltpu.VMEM((BLK, 256, GP), F32),
             pltpu.VMEM((BLK, 256, GP), F32),
             pltpu.VMEM((BLK, 256, 256), BF16),
@@ -411,7 +460,7 @@
             pltpu.VMEM((8, 8, GP), F32),
             pltpu.VMEM((8, 8, GP), F32),
             pltpu.VMEM((LIST, 8, GP), F32),
-            row(64), row(64), row(64), row(64),
+            row(128), row(128),
             pltpu.VMEM((8, 8, GP), F32),
             pltpu.VMEM((8, GP), F32),
             pltpu.VMEM((8, GP), F32),
@@ -422,7 +471,8 @@
         compiler_params=pltpu.CompilerParams(
             collective_id=0, has_side_effects=True, vmem_limit_bytes=32 << 20
         ),
-    )(fetch, lists, counts, cell_rank, params, d_rows)
+    )(hb(fetch), hb(lists), counts, hb(cell_rank), hb(params), hb(d_rows))
+    colour, grads = finish(colour, grads)
     return jnp.transpose(colour, (1, 0, 2)), jnp.transpose(grads, (1, 0, 2))
 
 

time: 45.5 us -> 39.9 us (0.88)
  Pallas kernels: 41.4 us -> 38.4 us
  local copies, waits for them, and re-layouts: 2.64 us -> 0 us
    pallas_call x1, Pallas kernels: 41.4 us -> 37.8 us  [body(): pl.pallas_call(kernel, out_shape=(jax.ShapeDtypeStruct((3, 1, 32), F32),...]
    unnamed x12 -> x0, local copies, waits for them, and re-layouts: 2.64 us -> none
    pallas_call x0 -> x1, Pallas kernels: none -> 0.64 us  [finish(): pl.pallas_call(put, out_shape=(jax.ShapeDtypeStruct(colour.shape, F32), j...]
where the time goes in v2:
time: 39.9 us; the launch traced here: 39.7 us
  Pallas kernels  38.4 us (96%)
  between operations  1.28 us (3%)
    pallas_call x1, Pallas kernels, body(): pl.pallas_call(kernel, out_shape=(jax.ShapeDtypeStruct((3, 1, 32), F32),...  37.8 us

profile of v2, /device:TPU:1, one launch (start us, length us, event | category | flops | bytes accessed | tf_op | source)
XLA Modules:
  0.0 39.7 jit_solution(18426274729215771010)
XLA Ops:
  1.3 37.8 %shard_map.77 = (f32[3,1,32]{2,1,0:T(1,128)S(1)}, f32[9,8,128]{2,1,0:T(8,128)S(1)}) custom-call(s32[4,64]{1,0:T(4,128)} %bitcast.9, s32[1,12]{1,0:T(1,128)} %bitcast.11, s32[1,1]{1,0:T(1,128)S(6)} %copy.8.count_h, s32[1,8]{1,0:T(1,128)} %rank_h.1, f32[9,8,128]{2,1,0:T(8,128)} %bitcast.8, f32[3,1,32]{2,1,0:T(1,128)} %bitcast.10), custom_call_target="tpu_custom_call" | custom-call | tf_op jit(solution)/shard_map/pallas_call | solution.py:432
  39.0 0.6 %shard_map.78 = (f32[3,1,32]{2,1,0:T(1,128)}, f32[9,8,128]{2,1,0:T(8,128)}) custom-call(f32[3,1,32]{2,1,0:T(1,128)S(1)} %get-tuple-element.6.colour_ref, f32[9,8,128]{2,1,0:T(8,128)S(1)} %get-tuple-element.7.grad_ref), custom_call_target="tpu_custom_call" | custom-call | tf_op jit(solution)/shard_map/pallas_call | solution.py:413

commit v3 on v2

--- a/solution.py
+++ b/solution.py
@@ -17,6 +17,8 @@
 BLK = 8
 GP = 128
 NPX = 4
+HEADS = 32
+HALVES = 2
 L_PEER, L_RANK, L_BLK, L_DCOL = 0, 16, 32, 64
 
 
@@ -46,7 +48,7 @@
     fetch_h, list_h, count_h, rank_h, g_h, dcol_h,
     colour_ref, grad_ref,
     fetch_s, list_s, count_s, rank_s, g_ref, dcol_ref, in_sem,
-    w_ref, u_ref, wsplit_ref, wcol_ref, crow_ref, mom_ref, dpad_ref,
+    w_ref, u_ref, wsplit_ref, wcol_ref, crow_ref, mom_ref, dpad_ref, rows_ref,
     fold_ref, unfold_ref, hot_ref, pick_ref, hot_t_ref, rank_ref, lit_ref, dens_ref,
     send_b, recv_b, all_x, send_d, recv_d, send_f, recv_f, send_c, recv_c,
     send_sem, recv_sem,
@@ -55,7 +57,10 @@
     own = lax.axis_index("own")
     own_y = lax.div(own, 8)
     own_z = lax.rem(own, 8)
-    holder = own_y == cell
+    head = own_z < 4
+    not_head = own_z >= 4
+    pair_of = 4 * own_y + own_z
+    holder = head & (own_y == cell)
 
     def far_first(visit):
         def pair(k, carry):
@@ -71,9 +76,13 @@
         lax.fori_loop(0, 7, near, 0)
 
     barrier = pltpu.get_barrier_semaphore()
-    far_first(lambda peer: pl.semaphore_signal(barrier, inc=1, device_id=(cell, peer), device_id_type=MESH))
-    for i in CELL_ORDER:
-        pl.semaphore_signal(barrier, inc=1, device_id=(lax.rem(cell + i, CELL), own), device_id_type=MESH)
+
+    @pl.when(head)
+    def _():
+        far_first(lambda peer: pl.semaphore_signal(barrier, inc=1, device_id=(cell, peer), device_id_type=MESH))
+        for i in CELL_ORDER:
+            pl.semaphore_signal(barrier, inc=1, device_id=(lax.rem(cell + i, CELL), own), device_id_type=MESH)
+
     loads = [
         pltpu.make_async_copy(source, target, in_sem.at[i])
         for i, (source, target) in enumerate(
@@ -112,9 +121,11 @@
         moved = jnp.where(of_row, pltpu.roll(slanted, L_DCOL - 4 * i, 1), 0.0)
         moved = jnp.broadcast_to(jnp.sum(moved, axis=0, keepdims=True), (8, GP))
         dcol_rows = jnp.where(row8 == i, moved, dcol_rows)
+    rows_ref[0:8, :] = dcol_rows
+    two_groups = rows_ref[pl.ds(0, 4, stride=2), :] + pltpu.roll(rows_ref[pl.ds(1, 4, stride=2), :], 16, 1)
     for i in range(8):
         mine = (cell == i).astype(F32)
-        send_b[pl.ds(16 * i + 1, 8, stride=2), :] = aux + mine * dcol_rows
+        send_b[pl.ds(16 * i + 2, 4, stride=4), :] = aux[0:4] + mine * two_groups
 
     mean_x, mean_y = g_ref[0], g_ref[1]
     inv_a, inv_c = jnp.exp(g_ref[2]), jnp.exp(g_ref[3])
@@ -165,158 +176,207 @@
     rows = total[0:64]
     for r in range(1, NPX):
         rows += pltpu.roll(total[64 * r : 64 * r + 64], 32 * r, 1)
-    send_b[pl.ds(0, 64, stride=2), :] = rows
-
-    pl.semaphore_wait(barrier, OWN - 1 + CELL - 1)
-
-    def spread_rows(source, target, rows, slot):
-        def one(peer):
+    rows_ref[...] = rows
+    for h in range(HALVES):
+        send_b[pl.ds(h, HEADS, stride=4), :] = rows_ref[pl.ds(h, HEADS, stride=2), :]
+
+    pl.semaphore_wait(barrier, jnp.where(head, HEADS - 1 + CELL - 1, HEADS))
+
+    def to_head(pair):
+        peer = pair + 4 * lax.div(pair, 4)
+
+        @pl.when(peer != own)
+        def _():
             pltpu.make_async_remote_copy(
-                source.at[pl.ds(rows * peer, rows)], target.at[pl.ds(rows * own, rows)],
-                send_sem.at[slot], recv_sem.at[slot], device_id=(cell, peer), device_id_type=MESH,
+                send_b.at[pl.ds(4 * pair, 3)], recv_b.at[pl.ds(4 * own, 3)], send_sem.at[0], recv_sem.at[0],
+                device_id=(cell, peer), device_id_type=MESH,
             ).start()
 
-        far_first(one)
-        for i in range(rows):
-            target[pl.ds(rows * own + i, 1), :] = source[pl.ds(rows * own + i, 1), :]
-
-    spread_rows(send_b, recv_b, 2, 0)
-
-    for a in range(8):
-        lane_in = iota((GP, GP), 0)
-        lane_out = iota((GP, GP), 1)
-        same = (lane_out // 16 == a) & (lane_out % 4 == lane_in // 32)
-        to_own = same & ((lane_out % 16) // 4 == lane_in % 4)
-        to_all = same & (lane_in % 4 == 3)
-        piece = jnp.concatenate([to_own.astype(F32), to_all.astype(F32)], axis=1).astype(BF16)
-        fold_ref[256 * a : 256 * a + 128, :] = piece
-        fold_ref[256 * a + 128 : 256 * a + 256, :] = piece
-        back = (lane_in // 16 == a) & (lane_in % 4 == lane_out // 32) & ((lane_in % 16) // 4 == lane_out % 4)
-        back = back.astype(F32).astype(BF16)
-        unfold_ref[0:128, 128 * a : 128 * a + 128] = back
-        unfold_ref[128:256, 128 * a : 128 * a + 128] = back
-
-    choose_in = iota((GP, 256), 0)
-    choose_out = iota((GP, 256), 1)
-    choose = (choose_in < 16) & (choose_out < 128) | (choose_in >= 32) & (choose_in < 48) & (choose_out >= 128)
-    choose = choose.astype(F32).astype(BF16)
-    wait_rows(recv_b, 2 * (OWN - 1), recv_sem.at[0])
-    lane8f = lane8.astype(F32)
-    block8f = ((lane8 // 4) % 8).astype(F32)
-    dense_d = jnp.zeros((8, GP), F32)
-    dense_r = jnp.zeros((8, GP), F32)
-    lone = []
-    for a in range(8):
-        tile_rows = recv_b[pl.ds(16 * a + 1, 8, stride=2), :]
-        here = lane8 // 16 == a
-        dense_d = jnp.where(here, pltpu.roll(tile_rows, (16 * a - L_DCOL) % GP, 1), dense_d)
-        dense_r = jnp.where(here, pltpu.roll(tile_rows, (16 * a - L_RANK) % GP, 1), dense_r)
-        for entry in range(LIST):
-            mine = (lane8 == L_PEER + entry) | (lane8 == L_BLK + entry)
-            lone.append(jnp.where(mine, tile_rows, 0.0))
-    named = mm(jnp.concatenate(lone, axis=0).astype(BF16), choose).reshape(96, 8, 256)
-    hot = jnp.where(named[:, :, 0:128] == lane8f[None], 1.0, 0.0).reshape(768, GP)
-    pick = jnp.where(named[:, :, 128:256] == block8f[None], 1.0, 0.0).reshape(768, GP).astype(BF16)
-    hot_ref[...] = hot
-    pick_ref[...] = pick
-    dense_d = jnp.where(chan8 < 3, dense_d, 0.0)
-
-    @pl.when(holder)
-    def _():
-        send_d[...] = dense_d
-        recv_d[...] = dense_d
+    def to_two_heads(k, carry):
+        to_head(lax.rem(4 * own_y + 16 + k, HEADS))
+        to_head(lax.rem(4 * own_y + 47 - k, HEADS))
+        return carry
+
+    lax.fori_loop(0, HEADS // 2, to_two_heads, 0)
+
+    def composite():
+        for a in range(8):
+            lane_in = iota((GP, GP), 0)
+            lane_out = iota((GP, GP), 1)
+            same = (lane_out // 16 == a) & (lane_out % 4 == lane_in // 32)
+            to_own = same & ((lane_out % 16) // 4 == lane_in % 4)
+            to_all = same & (lane_in % 4 == 3)
+            piece = jnp.concatenate([to_own.astype(F32), to_all.astype(F32)], axis=1).astype(BF16)
+            fold_ref[256 * a : 256 * a + 128, :] = piece
+            fold_ref[256 * a + 128 : 256 * a + 256, :] = piece
+            back = (lane_in // 16 == a) & (lane_in % 4 == lane_out // 32) & ((lane_in % 16) // 4 == lane_out % 4)
+            back = back.astype(F32).astype(BF16)
+            unfold_ref[0:128, 128 * a : 128 * a + 128] = back
+            unfold_ref[128:256, 128 * a : 128 * a + 128] = back
+
+        choose_in = iota((GP, 256), 0)
+        choose_out = iota((GP, 256), 1)
+        choose = (choose_in < 16) & (choose_out < 128) | (choose_in >= 32) & (choose_in < 48) & (choose_out >= 128)
+        choose = choose.astype(F32).astype(BF16)
+        for i in range(3):
+            recv_b[pl.ds(4 * own + i, 1), :] = send_b[pl.ds(4 * pair_of + i, 1), :]
+        wait_rows(recv_b, 3 * (OWN - 1), recv_sem.at[0])
+        lane8f = lane8.astype(F32)
+        block8f = ((lane8 // 4) % 8).astype(F32)
+        dense_d = [jnp.zeros((8, GP), F32)] * HALVES
+        dense_r = jnp.zeros((8, GP), F32)
+        lone = []
+        for a in range(8):
+            tile_rows = recv_b[pl.ds(32 * a + 2, 8, stride=4), :]
+            here = lane8 // 16 == a
+            dense_d = [
+                jnp.where(here, pltpu.roll(tile_rows, (16 * a - L_DCOL - 16 * h) % GP, 1), dense_d[h]) for h in range(HALVES)
+            ]
+            dense_r = jnp.where(here, pltpu.roll(tile_rows, (16 * a - L_RANK) % GP, 1), dense_r)
+            for entry in range(LIST):
+                mine = (lane8 == L_PEER + entry) | (lane8 == L_BLK + entry)
+                lone.append(jnp.where(mine, tile_rows, 0.0))
+        named = mm(jnp.concatenate(lone, axis=0).astype(BF16), choose).reshape(96, 8, 256)
+        hot = jnp.where(named[:, :, 0:128] == lane8f[None], 1.0, 0.0).reshape(768, GP)
+        pick = jnp.where(named[:, :, 128:256] == block8f[None], 1.0, 0.0).reshape(768, GP).astype(BF16)
+        hot_ref[...] = hot
+        pick_ref[...] = pick
+        dense_d = [jnp.where(chan8 < 3, dense_d[h], 0.0) for h in range(HALVES)]
+
+        @pl.when(holder)
+        def _():
+            for h in range(HALVES):
+                send_d[h] = dense_d[h]
+                recv_d[h] = dense_d[h]
+            for i in CELL_ORDER:
+                pltpu.make_async_remote_copy(
+                    send_d, recv_d, send_sem.at[2], recv_sem.at[2],
+                    device_id=(lax.rem(cell + i, CELL), own), device_id_type=MESH,
+                ).start()
+
+        one_rank = jnp.concatenate([jnp.where(lane8 % 16 == c, dense_r, 0.0) for c in range(CELL)], axis=0)
+        group = (iota((GP, GP), 0) // 16 == iota((GP, GP), 1) // 16).astype(F32).astype(BF16)
+        rank_ref[...] = mm(one_rank.astype(BF16), group).reshape(8, 8, GP)
+
+        pieces = []
+        for h in range(HALVES):
+            pieces += split(recv_b[pl.ds(h, 64, stride=4), :])
+        taken = mm(hot.astype(BF16)[:, 0:64], jnp.concatenate(pieces, axis=1)).astype(BF16)
+        taken = taken * jnp.concatenate([pick] * 4, axis=1)
+        taken = jnp.concatenate(
+            [
+                jnp.concatenate([taken[96 * a : 96 * a + 96, 256 * h : 256 * h + 256] for a in range(8)], axis=1)
+                for h in range(HALVES)
+            ],
+            axis=0,
+        )
+        folded = mm(taken, fold_ref[...])
+        entry_c = folded[:, 0:128].reshape(HALVES, LIST, 8, GP)
+        entry_t = folded[:, 128:256].reshape(HALVES, LIST, 8, GP)
+        for h in range(HALVES):
+            ahead = jnp.zeros((8, GP), F32)
+            part = jnp.zeros((8, GP), F32)
+            for entry in range(LIST):
+                seen = jnp.exp(ahead)
+                dens_ref[h, entry] = seen
+                part += seen * entry_c[h, entry]
+                ahead += entry_t[h, entry]
+            all_x[cell, h] = jnp.where(chan8 < 3, part, ahead)
         for i in CELL_ORDER:
             pltpu.make_async_remote_copy(
-                send_d, recv_d, send_sem.at[2], recv_sem.at[2],
+                all_x.at[cell], all_x.at[cell], send_sem.at[3], recv_sem.at[3],
                 device_id=(lax.rem(cell + i, CELL), own), device_id_type=MESH,
             ).start()
 
-    one_rank = jnp.concatenate([jnp.where(lane8 % 16 == c, dense_r, 0.0) for c in range(CELL)], axis=0)
-    group = (iota((GP, GP), 0) // 16 == iota((GP, GP), 1) // 16).astype(F32).astype(BF16)
-    rank_ref[...] = mm(one_rank.astype(BF16), group).reshape(8, 8, GP)
-
-    s_hi, s_lo = split(recv_b[pl.ds(0, 64, stride=2), :])
-    taken = mm(hot.astype(BF16)[:, 0:64], jnp.concatenate([s_hi, s_lo], axis=1)).astype(BF16)
-    taken = taken * jnp.concatenate([pick, pick], axis=1)
-    taken = jnp.concatenate([taken[96 * a : 96 * a + 96] for a in range(8)], axis=1)
-    folded = mm(taken, fold_ref[...])
-    entry_c = folded[:, 0:128].reshape(LIST, 8, GP)
-    entry_t = folded[:, 128:256].reshape(LIST, 8, GP)
-    ahead = jnp.zeros((8, GP), F32)
-    part = jnp.zeros((8, GP), F32)
-    for entry in range(LIST):
-        seen = jnp.exp(ahead)
-        dens_ref[entry] = seen
-        part += seen * entry_c[entry]
-        ahead += entry_t[entry]
-    all_x[cell] = jnp.where(chan8 < 3, part, ahead)
-    for i in CELL_ORDER:
-        pltpu.make_async_remote_copy(
-            all_x.at[cell], all_x.at[cell], send_sem.at[3], recv_sem.at[3],
-            device_id=(lax.rem(cell + i, CELL), own), device_id_type=MESH,
-        ).start()
-
-    hot_t_ref[...] = hot_ref[...].T[0:64].astype(BF16)
-    ranks = [rank_ref[c] for c in range(CELL)]
-
-    @pl.when(jnp.logical_not(holder))
-    def _():
-        pltpu.make_async_copy(recv_d, recv_d, recv_sem.at[2]).wait()
-
-    wait_rows(all_x, CELL - 1, recv_sem.at[3])
-
-    dense_d = recv_d[...]
-    parts = [all_x[c] for c in range(CELL)]
-    logs, dots = [], []
-    for c in range(CELL):
-        last = jnp.where(chan8 == 3, parts[c], 0.0)
-        logs.append(last + pltpu.roll(last, 124, 1) + pltpu.roll(last, 120, 1) + pltpu.roll(last, 116, 1))
-        lossy = parts[c] * dense_d
-        dots.append(pltpu.roll(lossy, 4, 1) + pltpu.roll(lossy, 8, 1) + pltpu.roll(lossy, 12, 1))
-    colour = jnp.zeros((8, GP), F32)
-    behind = jnp.zeros((8, GP), F32)
-    my_rank = rank_ref[cell]
-    for c in range(CELL):
-        shade = jnp.zeros((8, GP), F32)
-        for other in range(CELL):
-            if other != c:
-                shade += jnp.where(ranks[other] < ranks[c], logs[other], 0.0)
-        lit = jnp.exp(shade)
-        lit_ref[c] = lit
-        colour += lit * parts[c]
-        behind += jnp.where(ranks[c] > my_rank, lit * dots[c], 0.0)
-    d_part = dense_d * lit_ref[cell]
-    grad_rows = [None] * LIST
-    for entry in reversed(range(LIST)):
-        d_c = dens_ref[entry] * d_part
-        grad_rows[entry] = jnp.where(chan8 < 3, d_c, behind)
-        lossy = d_c * entry_c[entry]
-        behind = behind + (pltpu.roll(lossy, 4, 1) + pltpu.roll(lossy, 8, 1) + pltpu.roll(lossy, 12, 1))
-    pick = pick_ref[...]
-    g_hi, g_lo = split(jnp.concatenate(grad_rows, axis=0))
-    wide = mm(jnp.concatenate([g_hi, g_lo], axis=1), unfold_ref[...])
-    wide = jnp.concatenate([wide[:, 128 * a : 128 * a + 128] for a in range(8)], axis=0)
-    wide_hi, wide_lo = split(wide)
-    wide = jnp.concatenate([wide_hi * pick, wide_lo * pick], axis=1)
-    back = mm(hot_t_ref[...], wide)
-    send_f[...] = back[:, 0:128] + back[:, 128:256]
-    spread_rows(send_f, recv_f, 1, 4)
-
-    for a in range(8):
-        send_c[8 * a : 8 * a + 8, :] = pltpu.roll(colour, (GP - 16 * a) % GP, 1)
-
-    @pl.when(holder)
-    def _():
+        hot_t_ref[...] = hot_ref[...].T[0:64].astype(BF16)
+        ranks = [rank_ref[c] for c in range(CELL)]
+
+        @pl.when(jnp.logical_not(holder))
+        def _():
+            pltpu.make_async_copy(recv_d, recv_d, recv_sem.at[2]).wait()
+
+        wait_rows(all_x, CELL - 1, recv_sem.at[3])
+
+        grad_rows = []
+        colours = []
+        my_rank = rank_ref[cell]
+        for h in range(HALVES):
+            dense = recv_d[h]
+            parts = [all_x[c, h] for c in range(CELL)]
+            logs, dots = [], []
+            for c in range(CELL):
+                last = jnp.where(chan8 == 3, parts[c], 0.0)
+                logs.append(last + pltpu.roll(last, 124, 1) + pltpu.roll(last, 120, 1) + pltpu.roll(last, 116, 1))
+                lossy = parts[c] * dense
+                dots.append(pltpu.roll(lossy, 4, 1) + pltpu.roll(lossy, 8, 1) + pltpu.roll(lossy, 12, 1))
+            colour = jnp.zeros((8, GP), F32)
+            behind = jnp.zeros((8, GP), F32)
+            for c in range(CELL):
+                shade = jnp.zeros((8, GP), F32)
+                for other in range(CELL):
+                    if other != c:
+                        shade += jnp.where(ranks[other] < ranks[c], logs[other], 0.0)
+                lit = jnp.exp(shade)
+                lit_ref[h, c] = lit
+                colour += lit * parts[c]
+                behind += jnp.where(ranks[c] > my_rank, lit * dots[c], 0.0)
+            colours.append(colour)
+            d_part = dense * lit_ref[h, cell]
+            of_half = [None] * LIST
+            for entry in reversed(range(LIST)):
+                d_c = dens_ref[h, entry] * d_part
+                of_half[entry] = jnp.where(chan8 < 3, d_c, behind)
+                lossy = d_c * entry_c[h, entry]
+                behind = behind + (pltpu.roll(lossy, 4, 1) + pltpu.roll(lossy, 8, 1) + pltpu.roll(lossy, 12, 1))
+            grad_rows += of_half
+        pick = pick_ref[...]
+        g_hi, g_lo = split(jnp.concatenate(grad_rows, axis=0))
+        wide = mm(jnp.concatenate([g_hi, g_lo], axis=1), unfold_ref[...])
+        columns = []
+        for h in range(HALVES):
+            spread = jnp.concatenate([wide[96 * h : 96 * h + 96, 128 * a : 128 * a + 128] for a in range(8)], axis=0)
+            spread_hi, spread_lo = split(spread)
+            columns += [spread_hi * pick, spread_lo * pick]
+        back = mm(hot_t_ref[...], jnp.concatenate(columns, axis=1))
+        for h in range(HALVES):
+            send_f[pl.ds(h, 64, stride=2), :] = back[:, 256 * h : 256 * h + 128] + back[:, 256 * h + 128 : 256 * h + 256]
         far_first(
             lambda peer: pltpu.make_async_remote_copy(
-                send_c.at[pl.ds(peer, 1)], recv_c.at[pl.ds(own_z, 1)], send_sem.at[5], recv_sem.at[5],
+                send_f.at[pl.ds(2 * peer, 2)], recv_f.at[pl.ds(2 * pair_of, 2)], send_sem.at[4], recv_sem.at[4],
                 device_id=(cell, peer), device_id_type=MESH,
             ).start()
         )
-        recv_c[pl.ds(own_z, 1), :] = send_c[pl.ds(own, 1), :]
+        for i in range(HALVES):
+            recv_f[pl.ds(2 * pair_of + i, 1), :] = send_f[pl.ds(2 * own + i, 1), :]
+
+        @pl.when(holder)
+        def _():
+            for h in range(HALVES):
+                for a in range(8):
+                    send_c[pl.ds(16 * a + h, 8, stride=2), :] = pltpu.roll(colours[h], (GP - 16 * a) % GP, 1)
+            far_first(
+                lambda peer: pltpu.make_async_remote_copy(
+                    send_c.at[pl.ds(2 * peer, 2)], recv_c.at[pl.ds(2 * own_z, 2)], send_sem.at[5], recv_sem.at[5],
+                    device_id=(cell, peer), device_id_type=MESH,
+                ).start()
+            )
+            for i in range(HALVES):
+                recv_c[pl.ds(2 * own_z + i, 1), :] = send_c[pl.ds(2 * own + i, 1), :]
+
+    @pl.when(head)
+    def _():
+        composite()
 
     after_of = (iota((2 * GP, GP), 0) % GP > iota((2 * GP, GP), 1)).astype(F32).astype(BF16)
-    wait_rows(recv_f, OWN - 1, recv_sem.at[4])
+
+    @pl.when(head)
+    def _():
+        wait_rows(recv_f, OWN - 2, recv_sem.at[4])
+
+    @pl.when(not_head)
+    def _():
+        wait_rows(recv_f, OWN, recv_sem.at[4])
+
     cot = recv_f[...]
     cot_hi = cot.astype(BF16).astype(F32)
     cot_lo = cot - cot_hi
@@ -376,7 +436,7 @@
 
     @pl.when(holder)
     def _():
-        wait_rows(recv_c, 7, recv_sem.at[5])
+        wait_rows(recv_c, 6, recv_sem.at[5])
 
     @pl.when(jnp.logical_not(holder))
     def _():
@@ -388,13 +448,19 @@
         moved = jnp.where(lane8 // 4 == row8, moved, 0.0)
         colour_ref[k] = jnp.sum(moved, axis=0, keepdims=True)[:, 0:32]
 
-    wait_rows(send_b, 2 * (OWN - 1), send_sem.at[0])
-    wait_rows(send_f, OWN - 1, send_sem.at[4])
-    wait_rows(all_x, CELL - 1, send_sem.at[3])
+    @pl.when(head)
+    def _():
+        wait_rows(send_b, 3 * (HEADS - 1), send_sem.at[0])
+        wait_rows(send_f, 2 * (OWN - 1), send_sem.at[4])
+        wait_rows(all_x, CELL - 1, send_sem.at[3])
+
+    @pl.when(not_head)
+    def _():
+        wait_rows(send_b, 3 * HEADS, send_sem.at[0])
 
     @pl.when(holder)
     def _():
-        wait_rows(send_c, OWN - 1, send_sem.at[5])
+        wait_rows(send_c, 2 * (OWN - 1), send_sem.at[5])
         wait_rows(all_x, CELL - 1, send_sem.at[2])
 
 
@@ -452,19 +518,20 @@
             pltpu.VMEM((32, GP), F32),
             pltpu.VMEM((6, 8, GP), F32),
             pltpu.VMEM((8, GP), F32),
+            pltpu.VMEM((64, GP), F32),
             pltpu.VMEM((2048, 256), BF16),
             pltpu.VMEM((256, 1024), BF16),
             pltpu.VMEM((768, GP), F32),
             pltpu.VMEM((768, GP), BF16),
             pltpu.VMEM((64, 768), BF16),
             pltpu.VMEM((8, 8, GP), F32),
-            pltpu.VMEM((8, 8, GP), F32),
-            pltpu.VMEM((LIST, 8, GP), F32),
-            row(128), row(128),
-            pltpu.VMEM((8, 8, GP), F32),
-            pltpu.VMEM((8, GP), F32),
-            pltpu.VMEM((8, GP), F32),
-            row(64), row(64), row(64), row(8),
+            pltpu.VMEM((HALVES, 8, 8, GP), F32),
+            pltpu.VMEM((HALVES, LIST, 8, GP), F32),
+            row(128), row(256),
+            pltpu.VMEM((8, HALVES, 8, GP), F32),
+            pltpu.VMEM((HALVES, 8, GP), F32),
+            pltpu.VMEM((HALVES, 8, GP), F32),
+            row(128), row(64), row(128), row(8),
             pltpu.SemaphoreType.DMA((6,)),
             pltpu.SemaphoreType.DMA((6,)),
         ],

time: 39.9 us -> 37 us (0.927)
  Pallas kernels: 38.4 us -> 35.6 us
    pallas_call x1, Pallas kernels: 37.8 us -> 34.9 us  [body(): pl.pallas_call(kernel, out_shape=(jax.ShapeDtypeStruct((3, 1, 32), F32),...]
where the time goes in v3:
time: 37 us; the launch traced here: 36.8 us
  Pallas kernels  35.6 us (96%)
  between operations  1.28 us (3%)
    pallas_call x1, Pallas kernels, body(): pl.pallas_call(kernel, out_shape=(jax.ShapeDtypeStruct((3, 1, 32), F32),...  34.9 us

profile of v3, /device:TPU:1, one launch (start us, length us, event | category | flops | bytes accessed | tf_op | source)
XLA Modules:
  0.0 36.8 jit_solution(1238426299502033492)
XLA Ops:
  1.3 34.9 %shard_map.77 = (f32[3,1,32]{2,1,0:T(1,128)S(1)}, f32[9,8,128]{2,1,0:T(8,128)S(1)}) custom-call(s32[4,64]{1,0:T(4,128)} %bitcast.9, s32[1,12]{1,0:T(1,128)} %bitcast.11, s32[1,1]{1,0:T(1,128)S(6)} %copy.8.count_h, s32[1,8]{1,0:T(1,128)} %rank_h.1, f32[9,8,128]{2,1,0:T(8,128)} %bitcast.8, f32[3,1,32]{2,1,0:T(1,128)} %bitcast.10), custom_call_target="tpu_custom_call" | custom-call | tf_op jit(solution)/shard_map/pallas_call | solution.py:498
  36.2 0.6 %shard_map.78 = (f32[3,1,32]{2,1,0:T(1,128)}, f32[9,8,128]{2,1,0:T(8,128)}) custom-call(f32[3,1,32]{2,1,0:T(1,128)S(1)} %get-tuple-element.6.colour_ref, f32[9,8,128]{2,1,0:T(8,128)S(1)} %get-tuple-element.7.grad_ref), custom_call_target="tpu_custom_call" | custom-call | tf_op jit(solution)/shard_map/pallas_call | solution.py:479

commit v4 on v3

--- a/solution.py
+++ b/solution.py
@@ -19,6 +19,7 @@
 NPX = 4
 HEADS = 32
 HALVES = 2
+LOG2E = 1.4426950408889634
 L_PEER, L_RANK, L_BLK, L_DCOL = 0, 16, 32, 64
 
 
@@ -57,10 +58,14 @@
     own = lax.axis_index("own")
     own_y = lax.div(own, 8)
     own_z = lax.rem(own, 8)
-    head = own_z < 4
-    not_head = own_z >= 4
-    pair_of = 4 * own_y + own_z
-    holder = head & (own_y == cell)
+    moved_in = (own_y == 0) & (own_z >= 4)
+    moved_out = (own_z == 3) & (own_y >= 3) & (own_y <= 6)
+    head = (own_z < 4) & jnp.logical_not(moved_out) | moved_in
+    not_head = jnp.logical_not(head)
+    pair_y = jnp.where(moved_in, own_z - 1, own_y)
+    pair_z = jnp.where(moved_in, 3, lax.rem(own_z, 4))
+    pair_of = 4 * pair_y + pair_z
+    holder = head & (pair_y == cell)
 
     def far_first(visit):
         def pair(k, carry):
@@ -74,6 +79,18 @@
 
         lax.fori_loop(0, 28, pair, 0)
         lax.fori_loop(0, 7, near, 0)
+
+    def early_first(visit):
+        def one(k, carry):
+            peer = 8 * lax.rem(own_y + 4 + lax.rem(k, 8), 8) + lax.div(k, 8)
+
+            @pl.when(peer != own)
+            def _():
+                visit(peer)
+
+            return carry
+
+        lax.fori_loop(0, OWN, one, 0)
 
     barrier = pltpu.get_barrier_semaphore()
 
@@ -137,42 +154,38 @@
         crow_ref[pl.ds(k, 8, stride=4), :] = g_ref[6 + k]
     crow = crow_ref[...]
     row32 = iota((32, GP), 0)
-    before_of = (iota((2 * GP, GP), 0) % GP < iota((2 * GP, GP), 1)).astype(F32).astype(BF16)
+    before_of = (iota((2 * GP, 2 * GP), 0) % GP < iota((2 * GP, 2 * GP), 1)).astype(F32).astype(BF16)
+    log_op = LOG2E * jnp.log(opacity)
+    half_a, half_c, cross2 = (0.5 * LOG2E) * inv_a, (0.5 * LOG2E) * inv_c, LOG2E * cross
     xs = [(4 * (row8 % 4) + r).astype(F32) + 0.5 for r in range(NPX)]
     ys = (2 * iota((8, 8, GP), 0) + iota((8, 8, GP), 1) // 4).astype(F32) + 0.5
 
+    lane256 = iota((256, GP), 1)
     total = jnp.zeros((256, 64), F32)
+    logs = jnp.zeros((256, GP), F32)
     for b in range(BLK):
         of = lambda v: jnp.broadcast_to(v[b : b + 1, :], (8, GP))
-        mx, my, ca, cc, cb, op = (of(v) for v in (mean_x, mean_y, inv_a, inv_c, cross, opacity))
+        mx, my, ca, cc, cb, op = (of(v) for v in (mean_x, mean_y, half_a, half_c, cross2, log_op))
         dy = ys - my[None]
-        part_y = (-0.5 * cc)[None] * dy * dy
+        part_y = op[None] - cc[None] * dy * dy
         slope = cb[None] * dy
         covs = []
         for r in range(NPX):
             dx = xs[r] - mx
-            covs.append(op[None] * jnp.exp(part_y - (0.5 * ca * dx * dx)[None] - dx[None] * slope))
+            covs.append(jnp.exp2(part_y - (ca * dx * dx)[None] - dx[None] * slope))
         cov = jnp.stack(covs, axis=0).reshape(256, GP)
-        keep_log = jnp.log(1.0 - cov)
-        log_hi, log_lo = split(keep_log)
-        before = mm(jnp.concatenate([log_hi, log_lo], axis=1), before_of)
-        weight = jnp.exp(before) * cov
-        w_hi, w_lo = split(weight)
-        colour_b = jnp.where(row32 // 4 == b, crow, 0.0)
-        ones_b = jnp.where(row32 == 4 * b + 3, 1.0, 0.0).astype(BF16)
-        c_hi, c_lo = split(colour_b)
-        none = jnp.zeros((32, GP), BF16)
-        top = jnp.concatenate([c_hi, ones_b], axis=1)
-        low = jnp.concatenate([c_lo, none], axis=1)
-        wcol_ref[b] = jnp.concatenate([top, low, top, jnp.concatenate([none, none], axis=1)], axis=0)
-        both = jnp.concatenate([top, low], axis=0)
-        total += mm_nt(jnp.concatenate([w_hi, log_hi], axis=1), both)
-        total += mm_nt(jnp.concatenate([w_lo, log_lo], axis=1), both)
+        before = mm(jnp.concatenate(split(jnp.log(1.0 - cov)), axis=1), before_of)
+        weight = jnp.exp(before[:, 0:GP]) * cov
+        logs = jnp.where(lane256 == 4 * b + 3, before[:, GP:], logs)
+        c_hi, c_lo = split(jnp.where(row32 // 4 == b, crow, 0.0))
+        both = jnp.concatenate(
+            [jnp.concatenate([c_hi, c_hi], axis=1), jnp.concatenate([c_lo, jnp.zeros((32, GP), BF16)], axis=1)], axis=0
+        )
+        total += mm_nt(jnp.concatenate(split(weight), axis=1), both)
         w_ref[b] = weight
-        u_ref[b] = cov * jnp.exp(-keep_log)
-        wsplit_ref[b] = jnp.concatenate([w_hi, w_lo], axis=1)
+        u_ref[b] = cov
     total = jnp.concatenate([total, jnp.zeros((256, 64), F32)], axis=1)
-    total = jnp.where(iota((256, GP), 1) < 32, total + pltpu.roll(total, 96, 1), 0.0)
+    total = jnp.where(lane256 < 32, total + pltpu.roll(total, 96, 1) + logs, 0.0)
     rows = total[0:64]
     for r in range(1, NPX):
         rows += pltpu.roll(total[64 * r : 64 * r + 64], 32 * r, 1)
@@ -183,7 +196,9 @@
     pl.semaphore_wait(barrier, jnp.where(head, HEADS - 1 + CELL - 1, HEADS))
 
     def to_head(pair):
-        peer = pair + 4 * lax.div(pair, 4)
+        row = lax.div(pair, 4)
+        late = (lax.rem(pair, 4) == 3) & (row >= 3) & (row <= 6)
+        peer = jnp.where(late, row + 1, pair + 4 * row)
 
         @pl.when(peer != own)
         def _():
@@ -198,6 +213,17 @@
         return carry
 
     lax.fori_loop(0, HEADS // 2, to_two_heads, 0)
+
+    for b in range(BLK):
+        cov = u_ref[b]
+        u_ref[b] = cov / (1.0 - cov)
+        wsplit_ref[b] = jnp.concatenate(split(w_ref[b]), axis=1)
+        ones_b = jnp.where(row32 == 4 * b + 3, 1.0, 0.0).astype(BF16)
+        c_hi, c_lo = split(jnp.where(row32 // 4 == b, crow, 0.0))
+        none = jnp.zeros((32, GP), BF16)
+        top = jnp.concatenate([c_hi, ones_b], axis=1)
+        low = jnp.concatenate([c_lo, none], axis=1)
+        wcol_ref[b] = jnp.concatenate([top, low, top, jnp.concatenate([none, none], axis=1)], axis=0)
 
     def composite():
         for a in range(8):
@@ -340,7 +366,7 @@
         back = mm(hot_t_ref[...], jnp.concatenate(columns, axis=1))
         for h in range(HALVES):
             send_f[pl.ds(h, 64, stride=2), :] = back[:, 256 * h : 256 * h + 128] + back[:, 256 * h + 128 : 256 * h + 256]
-        far_first(
+        early_first(
             lambda peer: pltpu.make_async_remote_copy(
                 send_f.at[pl.ds(2 * peer, 2)], recv_f.at[pl.ds(2 * pair_of, 2)], send_sem.at[4], recv_sem.at[4],
                 device_id=(cell, peer), device_id_type=MESH,
@@ -356,12 +382,12 @@
                     send_c[pl.ds(16 * a + h, 8, stride=2), :] = pltpu.roll(colours[h], (GP - 16 * a) % GP, 1)
             far_first(
                 lambda peer: pltpu.make_async_remote_copy(
-                    send_c.at[pl.ds(2 * peer, 2)], recv_c.at[pl.ds(2 * own_z, 2)], send_sem.at[5], recv_sem.at[5],
+                    send_c.at[pl.ds(2 * peer, 2)], recv_c.at[pl.ds(2 * pair_z, 2)], send_sem.at[5], recv_sem.at[5],
                     device_id=(cell, peer), device_id_type=MESH,
                 ).start()
             )
             for i in range(HALVES):
-                recv_c[pl.ds(2 * own_z + i, 1), :] = send_c[pl.ds(2 * own + i, 1), :]
+                recv_c[pl.ds(2 * pair_z + i, 1), :] = send_c[pl.ds(2 * own + i, 1), :]
 
     @pl.when(head)
     def _():

time: 37 us -> 35.4 us (0.957)
  Pallas kernels: 35.6 us -> 34 us
    pallas_call x1, Pallas kernels: 34.9 us -> 33.3 us  [body(): pl.pallas_call(kernel, out_shape=(jax.ShapeDtypeStruct((3, 1, 32), F32),...]
where the time goes in v4:
time: 35.4 us; the launch traced here: 35.2 us
  Pallas kernels  34 us (96%)
  between operations  1.28 us (4%)
    pallas_call x1, Pallas kernels, body(): pl.pallas_call(kernel, out_shape=(jax.ShapeDtypeStruct((3, 1, 32), F32),...  33.3 us

profile of v4, /device:TPU:1, one launch (start us, length us, event | category | flops | bytes accessed | tf_op | source)
XLA Modules:
  0.0 35.2 jit_solution(3761804330240414181)
XLA Ops:
  1.3 33.3 %shard_map.77 = (f32[3,1,32]{2,1,0:T(1,128)S(1)}, f32[9,8,128]{2,1,0:T(8,128)S(1)}) custom-call(s32[4,64]{1,0:T(4,128)} %bitcast.9, s32[1,12]{1,0:T(1,128)} %bitcast.11, s32[1,1]{1,0:T(1,128)S(6)} %copy.8.count_h, s32[1,8]{1,0:T(1,128)} %rank_h.1, f32[9,8,128]{2,1,0:T(8,128)} %bitcast.8, f32[3,1,32]{2,1,0:T(1,128)} %bitcast.10), custom_call_target="tpu_custom_call" | custom-call | tf_op jit(solution)/shard_map/pallas_call | solution.py:524
  34.6 0.6 %shard_map.78 = (f32[3,1,32]{2,1,0:T(1,128)}, f32[9,8,128]{2,1,0:T(8,128)}) custom-call(f32[3,1,32]{2,1,0:T(1,128)S(1)} %get-tuple-element.6.colour_ref, f32[9,8,128]{2,1,0:T(8,128)S(1)} %get-tuple-element.7.grad_ref), custom_call_target="tpu_custom_call" | custom-call | tf_op jit(solution)/shard_map/pallas_call | solution.py:505

commit v5 on v4

--- a/solution.py
+++ b/solution.py
@@ -233,8 +233,7 @@
             to_own = same & ((lane_out % 16) // 4 == lane_in % 4)
             to_all = same & (lane_in % 4 == 3)
             piece = jnp.concatenate([to_own.astype(F32), to_all.astype(F32)], axis=1).astype(BF16)
-            fold_ref[256 * a : 256 * a + 128, :] = piece
-            fold_ref[256 * a + 128 : 256 * a + 256, :] = piece
+            fold_ref[128 * a : 128 * a + 128, :] = piece
             back = (lane_in // 16 == a) & (lane_in % 4 == lane_out // 32) & ((lane_in % 16) // 4 == lane_out % 4)
             back = back.astype(F32).astype(BF16)
             unfold_ref[0:128, 128 * a : 128 * a + 128] = back
@@ -291,12 +290,13 @@
         taken = taken * jnp.concatenate([pick] * 4, axis=1)
         taken = jnp.concatenate(
             [
-                jnp.concatenate([taken[96 * a : 96 * a + 96, 256 * h : 256 * h + 256] for a in range(8)], axis=1)
-                for h in range(HALVES)
+                jnp.concatenate([taken[96 * a : 96 * a + 96, 128 * g : 128 * g + 128] for a in range(8)], axis=1)
+                for g in range(2 * HALVES)
             ],
             axis=0,
         )
-        folded = mm(taken, fold_ref[...])
+        folded = mm(taken, fold_ref[...]).reshape(HALVES, 2, 96, 256)
+        folded = (folded[:, 0] + folded[:, 1]).reshape(HALVES * 96, 256)
         entry_c = folded[:, 0:128].reshape(HALVES, LIST, 8, GP)
         entry_t = folded[:, 128:256].reshape(HALVES, LIST, 8, GP)
         for h in range(HALVES):
@@ -380,7 +380,7 @@
             for h in range(HALVES):
                 for a in range(8):
                     send_c[pl.ds(16 * a + h, 8, stride=2), :] = pltpu.roll(colours[h], (GP - 16 * a) % GP, 1)
-            far_first(
+            early_first(
                 lambda peer: pltpu.make_async_remote_copy(
                     send_c.at[pl.ds(2 * peer, 2)], recv_c.at[pl.ds(2 * pair_z, 2)], send_sem.at[5], recv_sem.at[5],
                     device_id=(cell, peer), device_id_type=MESH,
@@ -446,6 +446,7 @@
             myy += jnp.sum(qy * dy, axis=0)
         for i, m in enumerate((m0, mxs, mxx, mys, mxy, myy)):
             mom_ref[i, b : b + 1, :] = jnp.sum(m, axis=0, keepdims=True)
+    for b in range(BLK):
         grown = mm(turned, wsplit_ref[b])
         grown = grown[0:32, 0:128] + grown[0:32, 128:256] + grown[32:64, 0:128]
         d_colour = jnp.where(row32 // 4 == b, grown, d_colour)
@@ -545,7 +546,7 @@
             pltpu.VMEM((6, 8, GP), F32),
             pltpu.VMEM((8, GP), F32),
             pltpu.VMEM((64, GP), F32),
-            pltpu.VMEM((2048, 256), BF16),
+            pltpu.VMEM((1024, 256), BF16),
             pltpu.VMEM((256, 1024), BF16),
             pltpu.VMEM((768, GP), F32),
             pltpu.VMEM((768, GP), BF16),

time: 35.4 us -> 34.7 us (0.980)
  Pallas kernels: 34 us -> 33.2 us
    pallas_call x1, Pallas kernels: 33.3 us -> 32.6 us  [body(): pl.pallas_call(kernel, out_shape=(jax.ShapeDtypeStruct((3, 1, 32), F32),...]
where the time goes in v5:
time: 34.7 us; the launch traced here: 34.5 us
  Pallas kernels  33.2 us (96%)
  between operations  1.28 us (4%)
    pallas_call x1, Pallas kernels, body(): pl.pallas_call(kernel, out_shape=(jax.ShapeDtypeStruct((3, 1, 32), F32),...  32.6 us

profile of v5, /device:TPU:1, one launch (start us, length us, event | category | flops | bytes accessed | tf_op | source)
XLA Modules:
  0.0 34.5 jit_solution(14738953381550857360)
XLA Ops:
  1.3 32.6 %shard_map.77 = (f32[3,1,32]{2,1,0:T(1,128)S(1)}, f32[9,8,128]{2,1,0:T(8,128)S(1)}) custom-call(s32[4,64]{1,0:T(4,128)} %bitcast.9, s32[1,12]{1,0:T(1,128)} %bitcast.11, s32[1,1]{1,0:T(1,128)S(6)} %copy.8.count_h, s32[1,8]{1,0:T(1,128)} %rank_h.1, f32[9,8,128]{2,1,0:T(8,128)} %bitcast.8, f32[3,1,32]{2,1,0:T(1,128)} %bitcast.10), custom_call_target="tpu_custom_call" | custom-call | tf_op jit(solution)/shard_map/pallas_call | solution.py:525
  33.9 0.6 %shard_map.78 = (f32[3,1,32]{2,1,0:T(1,128)}, f32[9,8,128]{2,1,0:T(8,128)}) custom-call(f32[3,1,32]{2,1,0:T(1,128)S(1)} %get-tuple-element.6.colour_ref, f32[9,8,128]{2,1,0:T(8,128)S(1)} %get-tuple-element.7.grad_ref), custom_call_target="tpu_custom_call" | custom-call | tf_op jit(solution)/shard_map/pallas_call | solution.py:506
